TPU v7x, 256 devices: a whole 4x4x8 slice. The times are simulated.
256 devices in a mesh: batch: 4 (over x_lo, core), seq: 64 (over y, x_hi, z).
Axes of the slice: x: 4 (x_hi: 2, x_lo: 2; x = x_hi * 2 + x_lo), y: 4, z: 8, core: 2. Of those that a mesh axis runs over, the one named last changes fastest.
Arguments:
- signal: bfloat16 [4, 16384, 256], P('batch', 'seq'), may hold values from -0.125 to 0.125
- grad_out: bfloat16 [4, 16384, 256], P('batch', 'seq'), may hold values from -6 to 6
- filter_taps: float32 [16384, 256], P('seq'), may hold values from -0.125 to 0.125
- skip_gain: float32 [256], replicated, may hold values from 0.5 to 2
Outputs:
- input_grad: bfloat16 [4, 16384, 256], P('batch', 'seq')
- filter_grad: float32 [16384, 256], P('seq')
All inputs are finite; a program needn't handle non-finite values.
Results may differ from a plain program's by a relative error of at most 0.001.
Values sent between devices are 32-bit elements; how exact they have to be, the bound alone decides.
No kernel may reach another device: no remote copies, remote signals or barrier semaphores. Data moves between devices by JAX's collectives and lax.ppermute only.
A program may use at most 64 MiB of HBM per device.

v0:
```python
import jax
import jax.numpy as jnp
from jax import lax
from jax.sharding import PartitionSpec as P


def split_up(x, dim, devices):
    shape = x.shape
    parts = x.reshape(*shape[:dim], devices, shape[dim] // devices, *shape[dim + 1 :])
    return jnp.moveaxis(parts, dim, 0)


def summed_on_arrival(x, axis, dim):
    parts = split_up(x, dim, lax.axis_size(axis))
    arrived = lax.all_to_all(parts, axis, split_axis=0, concat_axis=0, tiled=True)
    return arrived.sum(axis=0)


def copy_for_each(x, axis):
    devices = lax.axis_size(axis)
    return lax.all_to_all(jnp.broadcast_to(x[None], (devices, *x.shape)), axis, 0, 0, tiled=True)


def in_order(parts, dim):
    shape = list(parts.shape[1:])
    shape[dim] *= parts.shape[0]
    return jnp.moveaxis(parts, 0, dim).reshape(shape)


def gather_directly(x, axis, dim):
    parts = copy_for_each(x, axis)
    return in_order(parts, dim)


def angle_table(height, width, period):
    product = lax.broadcasted_iota(jnp.int32, (height, width), 0) * lax.broadcasted_iota(
        jnp.int32, (height, width), 1
    )
    return 2.0 * jnp.pi / period * (product % period).astype(jnp.float32)


def angle_of(product, period):
    return 2.0 * jnp.pi / period * (product % period).astype(jnp.float32)


def coarse_order(slot, seq_count):
    pair_index = slot // 2
    odd_slot = slot % 2
    return jnp.where(
        pair_index == 0,
        odd_slot * seq_count,
        jnp.where(odd_slot == 0, pair_index, 2 * seq_count - pair_index),
    )


def contract(form, table, operand):
    return jnp.einsum(form, table, operand, precision=lax.Precision.HIGHEST)


def forward_spectra(columns):
    seq_count = lax.axis_size("seq")
    row_count = columns.shape[0]
    part_rows = row_count // seq_count
    period_len = 2 * row_count * seq_count
    spread = lax.all_to_all(
        columns.reshape(1, row_count, columns.shape[1]),
        "seq",
        split_axis=1,
        concat_axis=0,
        tiled=True,
    )
    slot_grid = lax.broadcasted_iota(jnp.int32, (2 * seq_count, seq_count), 0)
    source_grid = lax.broadcasted_iota(jnp.int32, (2 * seq_count, seq_count), 1)
    first_table = angle_of(coarse_order(slot_grid, seq_count) * source_grid, 2 * seq_count)
    cos_first = jnp.cos(first_table)
    sin_first = jnp.sin(first_table)
    half_width = spread.shape[2] // 2
    real_in = spread[:, :, :half_width]
    imag_in = spread[:, :, half_width:]
    real_part = contract("ks,srw->krw", cos_first, real_in) + contract(
        "ks,srw->krw", sin_first, imag_in
    )
    imag_part = contract("ks,srw->krw", cos_first, imag_in) - contract(
        "ks,srw->krw", sin_first, real_in
    )
    global_row = lax.axis_index("seq") * part_rows + lax.broadcasted_iota(
        jnp.int32, (2 * seq_count, part_rows), 1
    )
    coarse = coarse_order(lax.broadcasted_iota(jnp.int32, (2 * seq_count, part_rows), 0), seq_count)
    phases = angle_of(global_row * coarse, period_len)
    cos_turn = jnp.cos(phases)[:, :, None]
    sin_turn = jnp.sin(phases)[:, :, None]
    rotated = jnp.stack(
        [real_part * cos_turn + imag_part * sin_turn, imag_part * cos_turn - real_part * sin_turn]
    )
    inner_table = angle_table(row_count, row_count, row_count)
    cos_inner = jnp.cos(inner_table)
    sin_inner = jnp.sin(inner_table)
    pieces = lax.all_to_all(rotated, "seq", split_axis=1, concat_axis=2, tiled=True)
    real_sum = contract("qr,krw->kqw", cos_inner, pieces[0]) + contract(
        "qr,krw->kqw", sin_inner, pieces[1]
    )
    imag_sum = contract("qr,krw->kqw", cos_inner, pieces[1]) - contract(
        "qr,krw->kqw", sin_inner, pieces[0]
    )
    return jnp.stack([real_sum, imag_sum])


def split_pairs(packed):
    reversed_q = packed[:, :, ::-1]
    zero_row = jnp.roll(reversed_q[:, 0], 1, axis=1)
    own_pair = jnp.stack([zero_row, reversed_q[:, 1]], axis=1)
    partner = jnp.where(lax.axis_index("seq") == 0, own_pair, reversed_q[:, ::-1])
    first = jnp.stack([0.5 * (packed[0] + partner[0]), 0.5 * (packed[1] - partner[1])])
    second = jnp.stack([0.5 * (packed[1] + partner[1]), 0.5 * (partner[0] - packed[0])])
    return (first, second)


def inverse_rows(spectra):
    seq_count = lax.axis_size("seq")
    row_count = spectra.shape[2]
    period_len = 2 * row_count * seq_count
    inner_table = angle_table(row_count, row_count, row_count)
    cos_inner = jnp.cos(inner_table)
    sin_inner = jnp.sin(inner_table)
    real_sum = contract("qr,krw->kqw", cos_inner, spectra[0]) - contract(
        "qr,krw->kqw", sin_inner, spectra[1]
    )
    imag_sum = contract("qr,krw->kqw", cos_inner, spectra[1]) + contract(
        "qr,krw->kqw", sin_inner, spectra[0]
    )
    coarse = coarse_order(
        2 * lax.axis_index("seq") + lax.broadcasted_iota(jnp.int32, (2, row_count), 0), seq_count
    )
    position = lax.broadcasted_iota(jnp.int32, (2, row_count), 1)
    phases = angle_of(position * coarse, period_len)
    cos_turn = jnp.cos(phases)[:, :, None]
    sin_turn = jnp.sin(phases)[:, :, None]
    rotated = jnp.stack(
        [real_sum * cos_turn - imag_sum * sin_turn, real_sum * sin_turn + imag_sum * cos_turn]
    )
    target_grid = lax.broadcasted_iota(jnp.int32, (seq_count, 2 * seq_count), 0)
    slot_grid = lax.broadcasted_iota(jnp.int32, (seq_count, 2 * seq_count), 1)
    last_table = angle_of(target_grid * coarse_order(slot_grid, seq_count), 2 * seq_count)
    cos_last = jnp.cos(last_table)
    sin_last = jnp.sin(last_table)
    pieces = lax.all_to_all(rotated, "seq", split_axis=2, concat_axis=1, tiled=True)
    value = contract("sk,krw->srw", cos_last, pieces[0]) - contract(
        "sk,krw->srw", sin_last, pieces[1]
    )
    other = contract("sk,krw->srw", sin_last, pieces[0]) + contract(
        "sk,krw->srw", cos_last, pieces[1]
    )
    gathered = (value / period_len, other / period_len)
    gathered = jnp.concatenate([gathered[0], gathered[1]], axis=2)
    home_rows = lax.all_to_all(gathered, "seq", split_axis=0, concat_axis=1, tiled=True)
    return home_rows.reshape(row_count, home_rows.shape[2])


def invert_all(spectra):
    half_width = spectra.shape[3] // 2
    joined = jnp.stack(
        [
            spectra[0, :, :, :half_width] - spectra[1, :, :, half_width:],
            spectra[1, :, :, :half_width] + spectra[0, :, :, half_width:],
        ]
    )
    return inverse_rows(joined)


def shards(signal, grad_out, filter_taps, skip_gain):
    channels = filter_taps.shape[1]
    signal_rows = signal[0].astype(jnp.float32)
    grad_rows = grad_out[0].astype(jnp.float32)
    tap_half = filter_taps.shape[1] // 2
    columns = jnp.concatenate(
        [signal_rows, filter_taps[:, :tap_half], grad_rows, filter_taps[:, tap_half:]], axis=1
    )
    first, second = split_pairs(forward_spectra(columns))
    signal_spec = first[:, :, :, :channels]
    grad_spec = second[:, :, :, :channels]
    own_spec = jnp.concatenate([first[:, :, :, channels:], second[:, :, :, channels:]], axis=3)
    input_spec = jnp.stack(
        [
            grad_spec[0] * own_spec[0] + grad_spec[1] * own_spec[1],
            grad_spec[1] * own_spec[0] - grad_spec[0] * own_spec[1],
        ]
    )
    filter_terms = jnp.stack(
        [
            grad_spec[0] * signal_spec[0] + grad_spec[1] * signal_spec[1],
            grad_spec[1] * signal_spec[0] - grad_spec[0] * signal_spec[1],
        ]
    )
    shared_terms = summed_on_arrival(filter_terms, "batch", 3)
    rows_back = invert_all(jnp.concatenate([input_spec, shared_terms], axis=3))
    filter_grad = gather_directly(rows_back[:, channels:], "batch", 1)
    input_grad = (rows_back[:, :channels] + skip_gain[None, :] * grad_rows).astype(jnp.bfloat16)
    return (input_grad[None], filter_grad)


def solution(mesh):
    return jax.shard_map(
        shards,
        mesh=mesh,
        in_specs=(P("batch", "seq", None), P("batch", "seq", None), P("seq", None), P()),
        out_specs=(P("batch", "seq", None), P("seq", None)),
        check_vma=False,
    )
```

profile of v0, /device:TPU:1, one launch (start us, length us, event | category | flops | bytes accessed | tf_op | source)
XLA Modules:
  0.0 239.2 jit_solution(16720733413574259168)
XLA Ops:
  0.6 1.0 fusion.173
  1.6 1.0 bitcast_convert_fusion
  2.7 1.7 copy.29
  4.4 15.1 %all-to-all-start = ((f32[1,256,768]{2,0,1:T(1,128)}), f32[1,256,768]{2,0,1:T(1,128)S(1)}, u32[]{:S(2)}, u32[]{:S(2)}) async-start(f32[1,256,768]{2,0,1:T(1,128)} %copy.29), calls=%async_computation | async-start | bytes 1572864 | tf_op jit(solution)/shard_map/all_to_all | solution.py:65
  19.7 21.7 %all-to-all-done = f32[1,256,768]{2,0,1:T(1,128)S(1)} async-done(((f32[1,256,768]{2,0,1:T(1,128)}), f32[1,256,768]{2,0,1:T(1,128)S(1)}, u32[]{:S(2)}, u32[]{:S(2)}) %all-to-all-start) | async-done | bytes 786464 | tf_op jit(solution)/shard_map/all_to_all | solution.py:65
  41.4 1.9 reduce
  46.5 1.1 add_bitcast_fusion
  47.8 2.2 copy.32
  50.0 8.2 %all-to-all-start.1 = ((f32[2,128,4,384]{3,2,0,1:T(4,128)}), f32[2,128,4,384]{3,2,0,1:T(4,128)S(1)}, u32[]{:S(2)}, u32[]{:S(2)}) async-start(f32[2,128,4,384]{3,2,0,1:T(4,128)} %copy.32), calls=%async_computation.1 | async-start | bytes 3145728 | tf_op jit(solution)/shard_map/all_to_all | solution.py:99
  58.2 37.3 %all-to-all-done.1 = f32[2,128,4,384]{3,2,0,1:T(4,128)S(1)} async-done(((f32[2,128,4,384]{3,2,0,1:T(4,128)}), f32[2,128,4,384]{3,2,0,1:T(4,128)S(1)}, u32[]{:S(2)}, u32[]{:S(2)}) %all-to-all-start.1) | async-done | bytes 1572896 | tf_op jit(solution)/shard_map/all_to_all | solution.py:99
  97.4 1.8 fusion.35
  99.6 1.8 fusion.37
  101.4 1.8 convolution_add_fusion
  103.2 1.8 convolution_subtract_fusion
  105.0 1.3 fusion.4
  106.3 7.2 %slice.129 = f32[2,1,256,384]{2,3,0,1:T(8,128)} reverse(f32[2,1,256,384]{2,3,0,1:T(8,128)} %get-tuple-element.22), dimensions={2} | reverse | bytes 1572864 | tf_op jit(solution)/shard_map/slice | solution.py:111
  113.5 1.2 slice.158
  114.7 7.2 %slice.133 = f32[2,1,256,384]{2,3,1,0:T(8,128)} reverse(f32[2,1,256,384]{2,3,1,0:T(8,128)} %get-tuple-element.23), dimensions={2} | reverse | bytes 1572864 | tf_op jit(solution)/shard_map/slice | solution.py:112
  121.9 8.7 %rev.4 = f32[2,2,256,384]{2,3,1,0:T(8,128)} reverse(f32[2,2,256,384]{2,3,1,0:T(8,128)S(1)} %pad_maximum_fusion), dimensions={1,2} | reverse | bytes 3145728 | tf_op jit(solution)/shard_map/rev | solution.py:113
  130.6 1.5 maximum_bitcast_fusion.1
  132.3 1.3 maximum_select_fusion
  134.3 1.1 copy_bitcast_fusion.1
  135.4 8.5 %all-to-all-start.2 = ((f32[4,2,2,256,64]{3,4,2,1,0:T(8,128)}), f32[4,2,2,256,64]{3,4,2,1,0:T(8,128)S(1)}, u32[]{:S(2)}, u32[]{:S(2)}) async-start(f32[4,2,2,256,64]{3,4,2,1,0:T(8,128)} %copy_bitcast_fusion.1), calls=%async_computation.2 | async-start | bytes 2097152 | tf_op jit(solution)/shard_map/all_to_all | solution.py:15
  144.2 13.2 %all-to-all-done.2 = f32[4,2,2,256,64]{3,4,2,1,0:T(8,128)S(1)} async-done(((f32[4,2,2,256,64]{3,4,2,1,0:T(8,128)}), f32[4,2,2,256,64]{3,4,2,1,0:T(8,128)S(1)}, u32[]{:S(2)}, u32[]{:S(2)}) %all-to-all-start.2) | async-done | bytes 1048608 | tf_op jit(solution)/shard_map/all_to_all | solution.py:15
  157.6 1.4 fusion.31
  159.0 1.4 fusion.33
  160.4 1.4 convolution_add_fusion.2
  161.9 1.5 subtract_bitcast_fusion.1
  164.0 32.6 %all_to_all.61 = f32[2,2,256,160]{3,1,0,2:T(2,128)S(1)} all-to-all(f32[2,2,256,160]{3,1,0,2:T(2,128)S(1)} %copy.41), channel_id=1, replica_groups=mesh['batch'=4,'seq'=64] {'seq'}, dimensions={2} | all-to-all | bytes 1310720 | tf_op jit(solution)/shard_map/all_to_all | solution.py:147
  202.0 22.7 %all_to_all.62 = f32[64,4,320]{2,1,0:T(4,128)S(1)} all-to-all(f32[64,4,320]{2,1,0:T(4,128)S(1)} %copy.49), channel_id=1, replica_groups=mesh['batch'=4,'seq'=64] {'seq'}, dimensions={0} | all-to-all | bytes 655360 | tf_op jit(solution)/shard_map/all_to_all | solution.py:156
  225.6 7.7 %all-to-all-start.5 = ((f32[4,256,64]{1,2,0:T(8,128)}), f32[4,256,64]{1,2,0:T(8,128)S(1)}, u32[]{:S(2)}, u32[]{:S(2)}) async-start(f32[4,256,64]{1,2,0:T(8,128)} %broadcast_in_dim.5), calls=%async_computation.5 | async-start | bytes 524288 | tf_op jit(solution)/shard_map/all_to_all | solution.py:21
  234.0 4.3 %all-to-all-done.5 = f32[4,256,64]{1,2,0:T(8,128)S(1)} async-done(((f32[4,256,64]{1,2,0:T(8,128)}), f32[4,256,64]{1,2,0:T(8,128)S(1)}, u32[]{:S(2)}, u32[]{:S(2)}) %all-to-all-start.5) | async-done | bytes 262176 | tf_op jit(solution)/shard_map/all_to_all | solution.py:21
  (61 shorter events, 15.5 us)
Async XLA Ops:
  4.4 37.0 %all-to-all-start = ((f32[1,256,768]{2,0,1:T(1,128)}), f32[1,256,768]{2,0,1:T(1,128)S(1)}, u32[]{:S(2)}, u32[]{:S(2)}) async-start(f32[1,256,768]{2,0,1:T(1,128)} %copy.29), calls=%async_computation | async-start | bytes 1572864 | tf_op jit(solution)/shard_map/all_to_all | solution.py:65
  19.6 26.9 %copy-start.2 = (s32[128]{0:T(128)}, s32[128]{0:T(128)S(1)}, u32[]{:S(2)}) copy-start(s32[128]{0:T(128)S(1)} %get-tuple-element.44) | copy-start | bytes 1540
  19.6 26.9 %copy-start.4 = (s32[128]{0:T(128)}, s32[128]{0:T(128)S(1)}, u32[]{:S(2)}) copy-start(s32[128]{0:T(128)S(1)} %get-tuple-element.45) | copy-start | bytes 1540
  50.0 45.6 %all-to-all-start.1 = ((f32[2,128,4,384]{3,2,0,1:T(4,128)}), f32[2,128,4,384]{3,2,0,1:T(4,128)S(1)}, u32[]{:S(2)}, u32[]{:S(2)}) async-start(f32[2,128,4,384]{3,2,0,1:T(4,128)} %copy.32), calls=%async_computation.1 | async-start | bytes 3145728 | tf_op jit(solution)/shard_map/all_to_all | solution.py:99
  130.6 1.6 copy-start
  135.4 22.0 %all-to-all-start.2 = ((f32[4,2,2,256,64]{3,4,2,1,0:T(8,128)}), f32[4,2,2,256,64]{3,4,2,1,0:T(8,128)S(1)}, u32[]{:S(2)}, u32[]{:S(2)}) async-start(f32[4,2,2,256,64]{3,4,2,1,0:T(8,128)} %copy_bitcast_fusion.1), calls=%async_computation.2 | async-start | bytes 2097152 | tf_op jit(solution)/shard_map/all_to_all | solution.py:15
  197.0 0.8 copy-start.3
  197.0 0.8 copy-start.5
  202.0 31.3 %copy-start.1 = (bf16[1,256,256]{2,1,0:T(8,128)(2,1)S(1)}, bf16[1,256,256]{2,1,0:T(8,128)(2,1)}, u32[]{:S(2)}) copy-start(bf16[1,256,256]{2,1,0:T(8,128)(2,1)} %param.5) | copy-start | bytes 393220
  202.0 31.3 %copy-start.6 = (f32[256]{0:T(256)S(1)}, f32[256]{0:T(256)}, u32[]{:S(2)}) copy-start(f32[256]{0:T(256)} %param.7) | copy-start | bytes 3076
  225.6 12.7 %all-to-all-start.5 = ((f32[4,256,64]{1,2,0:T(8,128)}), f32[4,256,64]{1,2,0:T(8,128)S(1)}, u32[]{:S(2)}, u32[]{:S(2)}) async-start(f32[4,256,64]{1,2,0:T(8,128)} %broadcast_in_dim.5), calls=%async_computation.5 | async-start | bytes 524288 | tf_op jit(solution)/shard_map/all_to_all | solution.py:21
where the time goes:
time: 241 us; the launch traced here: 239 us
  waiting for transfers between devices  76.6 us (32%)
  blocking collectives  55.3 us (23%)
  starting transfers between devices  39.6 us (16%)
  local copies, waits for them, and re-layouts  36.1 us (15%)
  matrix products  20.2 us (8%)
  other arithmetic  10.4 us (4%)
    all_to_all x1, waiting for transfers between devices, forward_spectra(): lax.all_to_all(rotated, 'seq', split_axis=1, concat_axis=2, tiled=True)  37.3 us
    all_to_all x1, blocking collectives, inverse_rows(): lax.all_to_all(rotated, 'seq', split_axis=2, concat_axis=1, tiled=True)  32.6 us
    all_to_all x1, blocking collectives, inverse_rows(): lax.all_to_all(gathered, 'seq', split_axis=0, concat_axis=1, tiled=True)  22.7 us
    all_to_all x1, waiting for transfers between devices, forward_spectra(): lax.all_to_all(columns.reshape(1, row_count, columns.shape[1]), 'seq', sp...  21.7 us
    dot_general x16, matrix products, contract(): return jnp.einsum(form, table, operand, precision=lax.Precision.HIGHEST)  20.2 us
    all_to_all x1, starting transfers between devices, forward_spectra(): lax.all_to_all(columns.reshape(1, row_count, columns.shape[1]), 'seq', sp...  15.1 us
    all_to_all x1, waiting for transfers between devices, summed_on_arrival(): lax.all_to_all(parts, axis, split_axis=0, concat_axis=0, tiled=True)  13.2 us
    rev x1, local copies, waits for them, and re-layouts, split_pairs(): reversed_q[:, ::-1]  8.74 us
  transfers between devices with their start and end apart: 4, of which 4 were waited for; matrix products, arithmetic and copies ran while one was open for 0% of the time, Pallas kernels for 0%

commit v1 on v0

v1 whole, which is shorter than its diff:
```python
import functools

import jax
import jax.numpy as jnp
from jax import lax
from jax.experimental import pallas as pl
from jax.experimental.pallas import tpu as pltpu
from jax.sharding import PartitionSpec as P

LANES = 128
BLOCK = 256


def anti_identity(size):
    row = lax.broadcasted_iota(jnp.int32, (size, size), 0)
    column = lax.broadcasted_iota(jnp.int32, (size, size), 1)
    return jnp.where(row + column == size - 1, 1.0, 0.0).astype(jnp.bfloat16)


def product(left, right):
    return jnp.dot(left, right, preferred_element_type=jnp.float32)


def correlate(batch, blocks, got_ref, out_ref, hankel, flipped, u_left, h_left, total):
    tile = 5
    per_batch = BLOCK // batch
    flip_rows = anti_identity(blocks)
    flip_lanes = anti_identity(LANES)

    def rows_of(b, part):
        return got_ref[pl.ds(b * blocks * tile + part, blocks, stride=tile), :]

    def reversed_rows(values):
        turned = product(flip_rows, values.astype(jnp.bfloat16)).astype(jnp.bfloat16)
        return product(turned, flip_lanes)

    def spread(kind, left, base):
        for offset in range(16):
            for half in range(2):
                count = 2 * blocks - 16
                left[offset, base : base + count, half * LANES : (half + 1) * LANES] = flipped[
                    kind, half, pl.ds(offset, count), :
                ].astype(jnp.bfloat16)

    flipped[...] = jnp.zeros_like(flipped)
    halves = BLOCK // LANES
    pieces = LANES // per_batch
    for half in range(halves):
        taps = jnp.concatenate(
            [rows_of(half * pieces + piece, 4)[:, :per_batch] for piece in range(pieces)], axis=1
        )
        high = taps.astype(jnp.bfloat16).astype(jnp.float32)
        flipped[1, half, 0:blocks, :] = reversed_rows(high)
        flipped[2, half, 0:blocks, :] = reversed_rows(taps - high)
    count = 2 * blocks - 16
    spread(1, h_left, 0)
    spread(2, h_left, count)

    hankel[pl.ds(2 * blocks * LANES, LANES), :] = jnp.zeros((LANES, LANES), jnp.bfloat16)
    row = lax.broadcasted_iota(jnp.int32, (LANES, LANES), 0)
    lane = lax.broadcasted_iota(jnp.int32, (LANES, LANES), 1)
    own = lane <= row

    def turned(b, block):
        values = got_ref[pl.ds((b * blocks + block // 2) * tile + 2 + block % 2, 1), :]
        return pltpu.roll(jnp.broadcast_to(values, (LANES, LANES)), 1, 1, stride=1, stride_axis=0)

    def one_batch(b, carry):
        for half in range(halves):
            flipped[0, half, 0:blocks, :] = reversed_rows(rows_of(b, half))
        spread(0, u_left, 0)

        def build(step, current):
            for inner in range(2):
                block = 2 * step + inner
                following = turned(b, block + 1)
                hankel[pl.ds(block * LANES, LANES), :] = jnp.where(own, current, following).astype(
                    jnp.bfloat16
                )
                current = following
            return current

        current = lax.fori_loop(0, blocks - 1, build, turned(b, 0))
        block = 2 * blocks - 2
        following = turned(b, block + 1)
        hankel[pl.ds(block * LANES, LANES), :] = jnp.where(own, current, following).astype(
            jnp.bfloat16
        )
        hankel[pl.ds((block + 1) * LANES, LANES), :] = jnp.where(own, following, 0.0).astype(
            jnp.bfloat16
        )

        total[1] = jnp.zeros((blocks, BLOCK), jnp.float32)
        for group in range(blocks // 16):
            height = 16 * (group + 1)
            result = None
            for inner in range(16):
                k = 16 * group + inner
                start = blocks - 1 - k
                offset, base = start % 16, start - start % 16
                left = jnp.concatenate(
                    [
                        u_left[offset, base : base + height, :],
                        h_left[offset, base : base + height, :],
                        h_left[offset, count + base : count + base + height, :],
                    ],
                    axis=0,
                )
                right = jnp.concatenate(
                    [
                        hankel[k * BLOCK : (k + 1) * BLOCK, :],
                        hankel[k * BLOCK + LANES : (k + 1) * BLOCK + LANES, :],
                    ],
                    axis=1,
                )
                term = product(left, right)
                result = term if result is None else result + term
            total[0, 0:height, :] += result[0:height]
            total[1, 0:height, :] += result[height : 2 * height] + result[2 * height :]
        for half in range(halves):
            out_ref[pl.ds(b * blocks, blocks), half, :] = total[
                1, :, half * LANES : (half + 1) * LANES
            ]
        return carry

    total[0] = jnp.zeros((blocks, BLOCK), jnp.float32)
    lax.fori_loop(0, batch, one_batch, 0)
    for b in range(batch):
        for half in range(halves):
            out_ref[b * blocks : (b + 1) * blocks, 2 + half, :] = total[
                0, :, half * LANES : (half + 1) * LANES
            ]


def correlations(got, batch, blocks):
    count = 2 * blocks - 16
    return pl.pallas_call(
        functools.partial(correlate, batch, blocks),
        out_shape=jax.ShapeDtypeStruct((batch * blocks, 4, LANES), jnp.float32),
        in_specs=[pl.BlockSpec(memory_space=pltpu.VMEM)],
        out_specs=pl.BlockSpec(memory_space=pltpu.VMEM),
        scratch_shapes=[
            pltpu.VMEM(((2 * blocks + 1) * LANES, LANES), jnp.bfloat16),
            pltpu.VMEM((3, 2, 2 * blocks, LANES), jnp.float32),
            pltpu.VMEM((16, count, BLOCK), jnp.bfloat16),
            pltpu.VMEM((16, 2 * count, BLOCK), jnp.bfloat16),
            pltpu.VMEM((2, blocks, BLOCK), jnp.float32),
        ],
        cost_estimate=pl.CostEstimate(flops=6_000_000_000, bytes_accessed=2_000_000, transcendentals=0),
        name="correlate",
    )(got)


def shards(signal, grad_out, filter_taps, skip_gain):
    batch, blocks = lax.axis_size("batch"), lax.axis_size("seq")
    axes = ("batch", "seq")
    channels = filter_taps.shape[1]
    per_batch = BLOCK // batch
    grad_rows = grad_out[0].astype(jnp.float32)
    signal_rows = signal[0].astype(jnp.float32)
    taps = lax.dynamic_slice_in_dim(filter_taps, lax.axis_index("batch") * per_batch, per_batch, 0)
    sent = jnp.concatenate(
        [signal_rows.T, grad_rows.T, taps.T, jnp.zeros((channels, LANES - per_batch), jnp.float32)],
        axis=1,
    ).reshape(channels, 5, 1, LANES)
    got = lax.all_to_all(sent, axes, 0, 0, tiled=True)
    back = correlations(got.reshape(5 * channels, LANES), batch, blocks)
    home = lax.all_to_all(back, axes, 0, 0, tiled=True)
    input_conv = home[:, 0:2, :].reshape(channels, BLOCK).T
    filter_grad = home[:, 2:4, :].reshape(channels, BLOCK).T
    input_grad = (input_conv + skip_gain[None, :] * grad_rows).astype(jnp.bfloat16)
    return (input_grad[None], filter_grad)


def solution(mesh):
    return jax.shard_map(
        shards,
        mesh=mesh,
        in_specs=(P("batch", "seq", None), P("batch", "seq", None), P("seq", None), P()),
        out_specs=(P("batch", "seq", None), P("seq", None)),
        check_vma=False,
    )
```

time: 241 us -> 108 us (0.45)
  waiting for transfers between devices: 76.6 us -> 0 us
  starting transfers between devices: 39.6 us -> 0 us
  Pallas kernels: 0 us -> 37.7 us
  local copies, waits for them, and re-layouts: 36.1 us -> 3.14 us
  matrix products: 20.2 us -> 0 us
  blocking collectives: 55.3 us -> 64.7 us
  other arithmetic: 10.4 us -> 1.78 us
    all_to_all x4 -> x0, waiting for transfers between devices: 76.6 us -> none  [the longest x1 37.3 us: forward_spectra(): lax.all_to_all(rotated, 'seq', split_axis=1, concat_axis=2, tiled=True)]
    all_to_all x4 -> x0, starting transfers between devices: 39.6 us -> none  [the longest x1 15.1 us: forward_spectra(): lax.all_to_all(columns.reshape(1, row_count, columns.shape[1]), 'seq', sp...]
    pallas_call x0 -> x1, Pallas kernels: none -> 37.7 us  [correlations(): pl.pallas_call(functools.partial(correlate, batch, blocks), out_shape=jax...]
    dot_general x16 -> x0, matrix products: 20.2 us -> none  [contract(): return jnp.einsum(form, table, operand, precision=lax.Precision.HIGHEST)]
    slice x11 -> x1, local copies, waits for them, and re-layouts: 17.9 us -> 0.2 us  [shards(): filter_grad = home[:, 2:4, :].reshape(channels, BLOCK).T]
    all_to_all x2, blocking collectives: 55.3 us -> 64.7 us  [the longest x1 38.4 us: shards(): got = lax.all_to_all(sent, axes, 0, 0, tiled=True)]
    rev x1 -> x0, local copies, waits for them, and re-layouts: 8.74 us -> none  [split_pairs(): reversed_q[:, ::-1]]
    another operation x2 -> x0, local copies, waits for them, and re-layouts: 2.79 us -> none  [the longest x1 2.19 us: forward_spectra(): jnp.stack([real_part * cos_turn + imag_part * sin_turn, imag_part * cos_t...]
  transfers between devices with their start and end apart: 4 -> 0, of which waited for: 4 -> 0; matrix products, arithmetic and copies ran while one was open for 0% -> 0% of each run, Pallas kernels for 0% -> 0%
where the time goes in v1:
time: 108 us
  blocking collectives  64.7 us (60%)
  Pallas kernels  37.7 us (35%)
  local copies, waits for them, and re-layouts  3.14 us (3%)
  other arithmetic  1.78 us (2%)
    all_to_all x1, blocking collectives, shards(): got = lax.all_to_all(sent, axes, 0, 0, tiled=True)  38.4 us
    pallas_call x1, Pallas kernels, correlations(): pl.pallas_call(functools.partial(correlate, batch, blocks), out_shape=jax...  37.7 us
    all_to_all x1, blocking collectives, shards(): home = lax.all_to_all(back, axes, 0, 0, tiled=True)  26.3 us

profile of v1, /device:TPU:1, one launch (start us, length us, event | category | flops | bytes accessed | tf_op | source)
XLA Modules:
  0.0 108.0 jit_solution(18192854338937603918)
XLA Ops:
  0.6 0.0 copy-start
  0.6 0.0 copy-start.1
  0.7 0.1 pad.3.clone
  0.7 0.8 copy-done
  1.6 0.0 copy-done.1
  1.6 0.9 convert_bitcast_fusion
  2.6 0.1 maximum_maximum_fusion
  2.7 0.5 copy.15
  3.2 38.4 %all_to_all.10 = f32[256,5,1,128]{3,2,1,0:T(1,128)} all-to-all(f32[256,5,1,128]{3,2,1,0:T(1,128)S(1)} %copy.15), channel_id=1, replica_groups=mesh['batch'=4,'seq'=64] {'batch','seq'}, dimensions={0} | all-to-all | bytes 1310720 | tf_op jit(solution)/shard_map/all_to_all | solution.py:166
  41.6 37.7 %correlate.1 = f32[256,4,128]{2,1,0:T(4,128)} custom-call(f32[1280,128]{1,0:T(8,128)} %bitcast.24), custom_call_target="tpu_custom_call" | custom-call | flops 6000000000 | bytes 2000000 | tf_op jit(solution)/shard_map/correlate/pallas_call | solution.py:137
  79.2 26.3 %all_to_all.11 = f32[256,4,128]{2,1,0:T(4,128)S(1)} all-to-all(f32[256,4,128]{2,1,0:T(4,128)} %correlate.1), channel_id=1, replica_groups=mesh['batch'=4,'seq'=64] {'batch','seq'}, dimensions={0} | all-to-all | bytes 1048576 | tf_op jit(solution)/shard_map/all_to_all | solution.py:168
  105.5 0.2 fusion.2
  105.8 0.8 copy.17
  106.6 0.0 copy-start.2
  106.6 0.1 copy.16
  106.7 0.5 copy-done.2
  107.3 0.7 fusion.1
  (2 shorter events, 0.0 us)
Async XLA Ops:
  0.6 1.0 copy-start
  0.6 1.0 copy-start.1
  106.6 0.7 copy-start.2

commit v2 on v1

v2 whole, which is shorter than its diff:
```python
import functools

import jax
import jax.numpy as jnp
from jax import lax
from jax.experimental import pallas as pl
from jax.experimental.pallas import tpu as pltpu
from jax.sharding import PartitionSpec as P

LANES = 128
BLOCK = 256
PACK = 16


def anti_identity(size):
    row = lax.broadcasted_iota(jnp.int32, (size, size), 0)
    column = lax.broadcasted_iota(jnp.int32, (size, size), 1)
    return jnp.where(row + column == size - 1, 1.0, 0.0).astype(jnp.bfloat16)


def product(left, right):
    return jnp.dot(left, right, preferred_element_type=jnp.float32)


def correlate(batch, blocks, got_ref, out_ref, even, odd, flipped, u_left, h_left, total):
    tile = 5
    halves = BLOCK // LANES
    groups = blocks // PACK
    per_batch = BLOCK // batch
    flip_rows = anti_identity(blocks)
    flip_lanes = anti_identity(LANES)
    row = lax.broadcasted_iota(jnp.int32, (LANES, LANES), 0)
    lane = lax.broadcasted_iota(jnp.int32, (LANES, LANES), 1)
    nothing = jnp.zeros((LANES, LANES), jnp.float32)

    def rows_of(b, part):
        return got_ref[pl.ds(b * blocks * tile + part, blocks, stride=tile), :]

    def reversed_rows(values):
        turned = product(flip_rows, values.astype(jnp.bfloat16)).astype(jnp.bfloat16)
        return product(turned, flip_lanes)

    def spread(kind, left, base):
        for offset in range(PACK):
            for half in range(halves):
                left[offset, base : base + blocks, half * LANES : (half + 1) * LANES] = flipped[
                    kind, half, pl.ds(offset, blocks), :
                ].astype(jnp.bfloat16)

    def turned(b, block):
        values = got_ref[pl.ds((b * blocks + block // 2) * tile + 2 + block % 2, 1), :]
        return pltpu.roll(jnp.broadcast_to(values, (LANES, LANES)), 1, 1, stride=1, stride_axis=0)

    def build(b, group, hankel):
        count = 2 * PACK + 1
        first = 2 * PACK * group

        def at(block):
            return turned(b, block) if block < 2 * blocks else nothing

        current = at(first)
        for inner in range(count):
            following = at(first + inner + 1)
            hankel[inner * LANES : (inner + 1) * LANES, :] = jnp.where(
                lane <= row, current, following
            ).astype(jnp.bfloat16)
            current = following

    def multiply(group, hankel):
        height = PACK * (group + 1)
        base = blocks - height
        result = None
        for inner in range(PACK):
            offset = PACK - 1 - inner
            left = jnp.concatenate(
                [
                    u_left[offset, base:blocks, :],
                    h_left[offset, base:blocks, :],
                    h_left[offset, blocks + base : 2 * blocks, :],
                ],
                axis=0,
            )
            right = jnp.concatenate(
                [
                    hankel[inner * BLOCK : (inner + 1) * BLOCK, :],
                    hankel[inner * BLOCK + LANES : (inner + 1) * BLOCK + LANES, :],
                ],
                axis=1,
            )
            term = product(left, right)
            result = term if result is None else result + term
        total[0, 0:height, :] += result[0:height]
        total[1, 0:height, :] += result[height : 2 * height] + result[2 * height :]

    flipped[...] = jnp.zeros_like(flipped)
    pieces = LANES // per_batch
    for half in range(halves):
        taps = jnp.concatenate(
            [rows_of(half * pieces + piece, 4)[:, :per_batch] for piece in range(pieces)], axis=1
        )
        high = taps.astype(jnp.bfloat16).astype(jnp.float32)
        flipped[batch, half, 0:blocks, :] = reversed_rows(high)
        flipped[batch + 1, half, 0:blocks, :] = reversed_rows(taps - high)
        for b in range(batch):
            flipped[b, half, 0:blocks, :] = reversed_rows(rows_of(b, half))
    spread(batch, h_left, 0)
    spread(batch + 1, h_left, blocks)
    total[0] = jnp.zeros((blocks, BLOCK), jnp.float32)
    build(0, 0, even)

    def one_batch(b, carry):
        total[1] = jnp.zeros((blocks, BLOCK), jnp.float32)
        spread(b, u_left, 0)
        for group in range(groups):
            now, later = (even, odd) if group % 2 == 0 else (odd, even)
            if group + 1 < groups:
                build(b, group + 1, later)
            else:
                build(jnp.minimum(b + 1, batch - 1), 0, later)
            multiply(group, now)
        for half in range(halves):
            out_ref[pl.ds(b * blocks * 4 + half, blocks, stride=4), :] = total[
                1, :, half * LANES : (half + 1) * LANES
            ]
        return carry

    lax.fori_loop(0, batch, one_batch, 0)
    for b in range(batch):
        for half in range(halves):
            out_ref[pl.ds(b * blocks * 4 + 2 + half, blocks, stride=4), :] = total[
                0, :, half * LANES : (half + 1) * LANES
            ]


def correlations(got, batch, blocks):
    hankel = pltpu.VMEM(((2 * PACK + 1) * LANES, LANES), jnp.bfloat16)
    return pl.pallas_call(
        functools.partial(correlate, batch, blocks),
        out_shape=jax.ShapeDtypeStruct((batch * blocks * 4, LANES), jnp.float32),
        in_specs=[pl.BlockSpec(memory_space=pltpu.VMEM)],
        out_specs=pl.BlockSpec(memory_space=pltpu.VMEM),
        scratch_shapes=[
            hankel,
            hankel,
            pltpu.VMEM((batch + 2, 2, blocks + PACK, LANES), jnp.float32),
            pltpu.VMEM((PACK, blocks, BLOCK), jnp.bfloat16),
            pltpu.VMEM((PACK, 2 * blocks, BLOCK), jnp.bfloat16),
            pltpu.VMEM((2, blocks, BLOCK), jnp.float32),
        ],
        compiler_params=pltpu.CompilerParams(vmem_limit_bytes=24 * 1024 * 1024),
        cost_estimate=pl.CostEstimate(flops=6_000_000_000, bytes_accessed=2_000_000, transcendentals=0),
        name="correlate",
    )(got)


def shards(signal, grad_out, filter_taps, skip_gain):
    batch, blocks = lax.axis_size("batch"), lax.axis_size("seq")
    axes = ("batch", "seq")
    channels = filter_taps.shape[1]
    per_batch = BLOCK // batch
    grad_rows = grad_out[0].astype(jnp.float32)
    signal_rows = signal[0].astype(jnp.float32)
    taps = lax.dynamic_slice_in_dim(filter_taps, lax.axis_index("batch") * per_batch, per_batch, 0)
    sent = jnp.concatenate(
        [signal_rows.T, grad_rows.T, taps.T, jnp.zeros((channels, LANES - per_batch), jnp.float32)],
        axis=1,
    ).reshape(channels, 5, 1, LANES)
    got = lax.all_to_all(sent, axes, 0, 0, tiled=True)
    back = correlations(got.reshape(5 * channels, LANES), batch, blocks).reshape(channels, 4, LANES)
    home = lax.all_to_all(back, axes, 0, 0, tiled=True)
    input_conv = home[:, 0:2, :].reshape(channels, BLOCK).T
    filter_grad = home[:, 2:4, :].reshape(channels, BLOCK).T
    input_grad = (input_conv + skip_gain[None, :] * grad_rows).astype(jnp.bfloat16)
    return (input_grad[None], filter_grad)


def solution(mesh):
    return jax.shard_map(
        shards,
        mesh=mesh,
        in_specs=(P("batch", "seq", None), P("batch", "seq", None), P("seq", None), P()),
        out_specs=(P("batch", "seq", None), P("seq", None)),
        check_vma=False,
    )
```

time: 108 us -> 78.4 us (0.73)
  Pallas kernels: 37.7 us -> 8.25 us
    pallas_call x1, Pallas kernels: 37.7 us -> 8.25 us  [correlations(): pl.pallas_call(functools.partial(correlate, batch, blocks), out_shape=jax...]
where the time goes in v2:
time: 78.4 us; the launch traced here: 78.2 us
  blocking collectives  64.4 us (82%)
  Pallas kernels  8.25 us (11%)
  local copies, waits for them, and re-layouts  3.14 us (4%)
  other arithmetic  1.78 us (2%)
    all_to_all x1, blocking collectives, shards(): got = lax.all_to_all(sent, axes, 0, 0, tiled=True)  38.3 us
    all_to_all x1, blocking collectives, shards(): home = lax.all_to_all(back, axes, 0, 0, tiled=True)  26.1 us
    pallas_call x1, Pallas kernels, correlations(): pl.pallas_call(functools.partial(correlate, batch, blocks), out_shape=jax...  8.25 us

profile of v2, /device:TPU:1, one launch (start us, length us, event | category | flops | bytes accessed | tf_op | source)
XLA Modules:
  0.0 78.2 jit_solution(666213703391202772)
XLA Ops:
  0.6 0.0 copy-start
  0.6 0.0 copy-start.1
  0.7 0.1 pad.3.clone
  0.7 0.8 %copy-done = f32[256,256]{1,0:T(8,128)S(1)} copy-done((f32[256,256]{1,0:T(8,128)S(1)}, f32[256,256]{1,0:T(8,128)}, u32[]{:S(2)}) %copy-start) | copy-done | bytes 262168
  1.6 0.0 copy-done.1
  1.6 0.9 %convert_bitcast_fusion = (f32[256,256]{0,1:T(8,128)S(1)}, f32[256,256]{0,1:T(8,128)S(1)}) fusion(bf16[1,256,256]{2,1,0:T(8,128)(2,1)S(1)} %copy-done.1, bf16[1,256,256]{2,1,0:T(8,128)(2,1)} %param.4), kind=kLoop, calls=%fused_computation.2 | loop fusion | flops 131072 | bytes 786432 | tf_op jit(solution)/shard_map/transpose | solution.py:165
  2.6 0.1 maximum_maximum_fusion
  2.7 0.5 copy.15
  3.2 38.3 %all_to_all.10 = f32[256,5,1,128]{3,2,1,0:T(1,128)S(1)} all-to-all(f32[256,5,1,128]{3,2,1,0:T(1,128)S(1)} %copy.15), channel_id=1, replica_groups=mesh['batch'=4,'seq'=64] {'batch','seq'}, dimensions={0} | all-to-all | bytes 1310720 | tf_op jit(solution)/shard_map/all_to_all | solution.py:168
  41.5 8.2 %correlate.1 = f32[1024,128]{1,0:T(8,128)S(1)} custom-call(f32[1280,128]{1,0:T(8,128)S(1)} %bitcast.24), custom_call_target="tpu_custom_call" | custom-call | flops 6000000000 | bytes 2000000 | tf_op jit(solution)/shard_map/correlate/pallas_call | solution.py:137
  49.7 26.1 %all_to_all.11 = f32[256,4,128]{2,1,0:T(4,128)S(1)} all-to-all(f32[256,4,128]{2,1,0:T(4,128)S(1)} %bitcast.25), channel_id=1, replica_groups=mesh['batch'=4,'seq'=64] {'batch','seq'}, dimensions={0} | all-to-all | bytes 1048576 | tf_op jit(solution)/shard_map/all_to_all | solution.py:170
  75.8 0.2 fusion.2
  76.0 0.8 %copy.14 = f32[256,2,128]{0,2,1:T(8,128)} copy(f32[256,2,128]{2,1,0:T(2,128)S(1)} %get-tuple-element.2) | data formatting | bytes 524288 | tf_op jit(solution)/shard_map/slice | solution.py:172
  76.9 0.0 copy-start.2
  76.9 0.1 copy.13
  77.0 0.5 copy-done.2
  77.6 0.7 fusion.1
  (2 shorter events, 0.0 us)
Async XLA Ops:
  0.6 1.0 %copy-start = (f32[256,256]{1,0:T(8,128)S(1)}, f32[256,256]{1,0:T(8,128)}, u32[]{:S(2)}) copy-start(f32[256,256]{1,0:T(8,128)} %param.6) | copy-start | bytes 786436
  0.6 1.0 %copy-start.1 = (bf16[1,256,256]{2,1,0:T(8,128)(2,1)S(1)}, bf16[1,256,256]{2,1,0:T(8,128)(2,1)}, u32[]{:S(2)}) copy-start(bf16[1,256,256]{2,1,0:T(8,128)(2,1)} %param.5) | copy-start | bytes 393220
  76.9 0.7 copy-start.2

commit v3 on v2

v3 whole, which is shorter than its diff:
```python
import functools

import jax
import jax.numpy as jnp
from jax import lax
from jax.experimental import pallas as pl
from jax.experimental.pallas import tpu as pltpu
from jax.sharding import PartitionSpec as P

LANES = 128
ROWS = 8
BLOCK = 256
HALVES = BLOCK // LANES
PACK = 16
SENT = 5
BACK = 4


def product(left, right):
    return jnp.dot(left, right, preferred_element_type=jnp.float32)


def anti_identity(size):
    row = lax.broadcasted_iota(jnp.int32, (size, size), 0)
    column = lax.broadcasted_iota(jnp.int32, (size, size), 1)
    return jnp.where(row + column == size - 1, 1.0, 0.0).astype(jnp.bfloat16)


def correlate(batch, blocks, got_ref, out_ref, even, odd, flipped, h_left, total):
    groups = blocks // PACK
    per_batch = BLOCK // batch
    flip_lanes = anti_identity(LANES)
    row = lax.broadcasted_iota(jnp.int32, (LANES, LANES), 0)
    lane = lax.broadcasted_iota(jnp.int32, (LANES, LANES), 1)
    nothing = jnp.zeros((LANES, LANES), jnp.float32)
    gain = jnp.broadcast_to(got_ref[SENT - 1 : SENT, per_batch : per_batch + 1], (1, LANES))
    upward = ROWS - 1 - lax.broadcasted_iota(jnp.int32, (ROWS, LANES), 0)

    def rows_of(b, part):
        return got_ref[pl.ds(b * blocks * SENT + part, blocks, stride=SENT), :]

    def keep_flipped(kind, half, values):
        turned = product(values.astype(jnp.bfloat16), flip_lanes)
        for first in range(0, blocks, ROWS):
            flipped[kind, half, blocks - ROWS - first : blocks - first, :] = jnp.take_along_axis(
                turned[first : first + ROWS], upward, axis=0
            )
        flipped[kind, half, blocks : blocks + PACK, :] = jnp.zeros((PACK, LANES), jnp.float32)

    def spread(kind, left, base):
        for offset in range(PACK):
            for half in range(HALVES):
                left[offset, base : base + blocks, half * LANES : (half + 1) * LANES] = flipped[
                    kind, half, pl.ds(offset, blocks), :
                ].astype(jnp.bfloat16)

    def turned(b, block):
        values = got_ref[pl.ds((b * blocks + block // 2) * SENT + HALVES + block % 2, 1), :]
        return pltpu.roll(jnp.broadcast_to(values, (LANES, LANES)), 1, 1, stride=1, stride_axis=0)

    def build(b, group, hankel):
        count = 2 * PACK + 1
        first = 2 * PACK * group

        def at(block):
            return turned(b, block) if block < 2 * blocks else nothing

        current = at(first)
        for inner in range(count):
            following = at(first + inner + 1)
            hankel[inner * LANES : (inner + 1) * LANES, :] = jnp.where(
                lane <= row, current, following
            ).astype(jnp.bfloat16)
            current = following

    def multiply(b, group, hankel):
        height = PACK * (group + 1)
        base = blocks - height
        result = None
        for inner in range(PACK):
            offset = PACK - 1 - inner
            own = [
                flipped[b, half, pl.ds(base + offset, height), :].astype(jnp.bfloat16)
                for half in range(HALVES)
            ]
            left = jnp.concatenate(
                [
                    jnp.concatenate(own, axis=1),
                    h_left[offset, base:blocks, :],
                    h_left[offset, blocks + base : 2 * blocks, :],
                ],
                axis=0,
            )
            right = jnp.concatenate(
                [
                    hankel[inner * BLOCK : (inner + 1) * BLOCK, :],
                    hankel[inner * BLOCK + LANES : (inner + 1) * BLOCK + LANES, :],
                ],
                axis=1,
            )
            term = product(left, right)
            result = term if result is None else result + term
        total[0, 0:height, :] += result[0:height]
        total[1, 0:height, :] += result[height : 2 * height] + result[2 * height :]

    build(0, 0, even)
    pieces = LANES // per_batch
    for half in range(HALVES):
        taps = jnp.concatenate(
            [rows_of(half * pieces + piece, SENT - 1)[:, :per_batch] for piece in range(pieces)],
            axis=1,
        )
        high = taps.astype(jnp.bfloat16).astype(jnp.float32)
        keep_flipped(batch, half, high)
        keep_flipped(batch + 1, half, taps - high)
        for b in range(batch):
            keep_flipped(b, half, rows_of(b, half))
    spread(batch, h_left, 0)
    spread(batch + 1, h_left, blocks)
    total[0] = jnp.zeros((blocks, BLOCK), jnp.float32)

    def one_batch(b, last):
        total[1] = jnp.zeros((blocks, BLOCK), jnp.float32)
        for group in range(groups):
            now, later = (even, odd) if group % 2 == 0 else (odd, even)
            if group + 1 < groups:
                build(b, group + 1, later)
            elif not last:
                build(b + 1, 0, later)
            multiply(b, group, now)
        for half in range(HALVES):
            out_ref[pl.ds(b * blocks * BACK + half, blocks, stride=BACK), :] = (
                total[1, :, half * LANES : (half + 1) * LANES]
                + gain * rows_of(b, HALVES + half)
            )

    def step(b, carry):
        one_batch(b, False)
        return carry

    lax.fori_loop(0, batch - 1, step, 0)
    one_batch(batch - 1, True)
    for b in range(batch):
        for half in range(HALVES):
            out_ref[pl.ds(b * blocks * BACK + HALVES + half, blocks, stride=BACK), :] = total[
                0, :, half * LANES : (half + 1) * LANES
            ]


def correlations(got, batch, blocks):
    hankel = pltpu.VMEM(((2 * PACK + 1) * LANES, LANES), jnp.bfloat16)
    return pl.pallas_call(
        functools.partial(correlate, batch, blocks),
        out_shape=jax.ShapeDtypeStruct((batch * blocks * BACK, LANES), jnp.float32),
        in_specs=[pl.BlockSpec(memory_space=pltpu.VMEM)],
        out_specs=pl.BlockSpec(memory_space=pltpu.VMEM),
        scratch_shapes=[
            hankel,
            hankel,
            pltpu.VMEM((batch + 2, HALVES, blocks + PACK, LANES), jnp.float32),
            pltpu.VMEM((PACK, 2 * blocks, BLOCK), jnp.bfloat16),
            pltpu.VMEM((2, blocks, BLOCK), jnp.float32),
        ],
        compiler_params=pltpu.CompilerParams(vmem_limit_bytes=24 * 1024 * 1024),
        cost_estimate=pl.CostEstimate(flops=6_000_000_000, bytes_accessed=2_000_000, transcendentals=0),
        name="correlate",
    )(got)


def finish(home_ref, input_ref, filter_ref, own, shared, left):
    channels = filter_ref.shape[1]
    copies = []

    def send_home(source, target):
        copies.append(pltpu.make_async_copy(source, target, left.at[len(copies)]))
        copies[-1].start()

    for half in range(HALVES):
        rows = slice(half * LANES, (half + 1) * LANES)
        shared[rows, :] = home_ref[pl.ds(HALVES + half, channels, stride=BACK), :].T
        send_home(shared.at[rows, :], filter_ref.at[rows, :])
    for half in range(HALVES):
        rows = slice(half * LANES, (half + 1) * LANES)
        conv = home_ref[pl.ds(half, channels, stride=BACK), :].T
        own[0, rows, :] = conv.astype(jnp.bfloat16)
        send_home(own.at[:, rows, :], input_ref.at[:, rows, :])
    for copy in copies:
        copy.wait()


def gradients(home):
    channels = home.shape[0] // BACK
    vmem = pl.BlockSpec(memory_space=pltpu.VMEM)
    hbm = pl.BlockSpec(memory_space=pltpu.HBM)
    return pl.pallas_call(
        finish,
        out_shape=(
            jax.ShapeDtypeStruct((1, BLOCK, channels), jnp.bfloat16),
            jax.ShapeDtypeStruct((BLOCK, channels), jnp.float32),
        ),
        in_specs=[vmem],
        out_specs=(hbm, hbm),
        scratch_shapes=[
            pltpu.VMEM((1, BLOCK, channels), jnp.bfloat16),
            pltpu.VMEM((BLOCK, channels), jnp.float32),
            pltpu.SemaphoreType.DMA((2 * HALVES,)),
        ],
        compiler_params=pltpu.CompilerParams(vmem_limit_bytes=16 * 1024 * 1024),
        name="finish",
    )(home)


def shards(signal, grad_out, filter_taps, skip_gain):
    batch, blocks = lax.axis_size("batch"), lax.axis_size("seq")
    axes = ("batch", "seq")
    channels = filter_taps.shape[1]
    per_batch = BLOCK // batch
    grad_rows = grad_out[0].astype(jnp.float32)
    signal_rows = signal[0].astype(jnp.float32)
    gain = jnp.broadcast_to(skip_gain[:, None], (channels, LANES - per_batch))
    taps = lax.dynamic_slice_in_dim(filter_taps, lax.axis_index("batch") * per_batch, per_batch, 0)
    sent = jnp.concatenate(
        [signal_rows.T, grad_rows.T, taps.T, gain], axis=1
    ).reshape(channels, SENT, 1, LANES)
    got = lax.all_to_all(sent, axes, 0, 0, tiled=True)
    back = correlations(got.reshape(channels * SENT, LANES), batch, blocks)
    home = lax.all_to_all(back.reshape(channels, BACK, LANES), axes, 0, 0, tiled=True)
    return gradients(home.reshape(channels * BACK, LANES))


def solution(mesh):
    return jax.shard_map(
        shards,
        mesh=mesh,
        in_specs=(P("batch", "seq", None), P("batch", "seq", None), P("seq", None), P()),
        out_specs=(P("batch", "seq", None), P("seq", None)),
        check_vma=False,
    )
```

time: 78.4 us -> 76.2 us (0.972)
  local copies, waits for them, and re-layouts: 3.14 us -> 1.44 us
    slice x3 -> x0, local copies, waits for them, and re-layouts: 1.18 us -> none  [the longest x2 1.05 us: shards(): filter_grad = home[:, 2:4, :].reshape(channels, BLOCK).T]
    pallas_call x0 -> x1, Pallas kernels: none -> 0.87 us  [gradients(): pl.pallas_call(finish, out_shape=(jax.ShapeDtypeStruct((1, BLOCK, channel...]
where the time goes in v3:
time: 76.2 us; the launch traced here: 76 us
  blocking collectives  64.4 us (85%)
  Pallas kernels  8.53 us (11%)
  local copies, waits for them, and re-layouts  1.44 us (2%)
  other arithmetic  1 us (1%)
    all_to_all x1, blocking collectives, shards(): got = lax.all_to_all(sent, axes, 0, 0, tiled=True)  38.3 us
    all_to_all x1, blocking collectives, shards(): lax.all_to_all(back.reshape(channels, BACK, LANES), axes, 0, 0, tiled=True)  26.1 us
    pallas_call x1, Pallas kernels, correlations(): pl.pallas_call(functools.partial(correlate, batch, blocks), out_shape=jax...  7.66 us

profile of v3, /device:TPU:1, one launch (start us, length us, event | category | flops | bytes accessed | tf_op | source)
XLA Modules:
  0.0 76.0 jit_solution(3475698759630824085)
XLA Ops:
  0.6 0.0 copy-start
  0.6 0.0 copy-start.1
  0.7 0.9 %copy-done = f32[256,256]{1,0:T(8,128)S(1)} copy-done((f32[256,256]{1,0:T(8,128)S(1)}, f32[256,256]{1,0:T(8,128)}, u32[]{:S(2)}) %copy-start) | copy-done | bytes 262168
  1.6 0.0 copy-done.1
  1.6 0.0 copy-start.2
  1.6 1.0 %convert_bitcast_fusion = (f32[256,256]{0,1:T(8,128)S(1)}, f32[256,256]{0,1:T(8,128)S(1)}) fusion(bf16[1,256,256]{2,1,0:T(8,128)(2,1)S(1)} %copy-done.1, bf16[1,256,256]{2,1,0:T(8,128)(2,1)} %param.4), kind=kLoop, calls=%fused_computation.1 | loop fusion | flops 131072 | bytes 786432 | tf_op jit(solution)/shard_map/transpose | solution.py:223
  2.6 0.0 copy-done.2
  2.7 0.5 copy.9
  3.1 38.3 %all_to_all.10 = f32[256,5,1,128]{3,2,1,0:T(1,128)S(1)} all-to-all(f32[256,5,1,128]{3,2,1,0:T(1,128)S(1)} %copy.9), channel_id=1, replica_groups=mesh['batch'=4,'seq'=64] {'batch','seq'}, dimensions={0} | all-to-all | bytes 1310720 | tf_op jit(solution)/shard_map/all_to_all | solution.py:225
  41.4 7.7 %correlate.1 = f32[1024,128]{1,0:T(8,128)S(1)} custom-call(f32[1280,128]{1,0:T(8,128)S(1)} %bitcast.17), custom_call_target="tpu_custom_call" | custom-call | flops 6000000000 | bytes 2000000 | tf_op jit(solution)/shard_map/correlate/pallas_call | solution.py:152
  49.1 26.1 %all_to_all.11 = f32[256,4,128]{2,1,0:T(4,128)S(1)} all-to-all(f32[256,4,128]{2,1,0:T(4,128)S(1)} %bitcast.18), channel_id=1, replica_groups=mesh['batch'=4,'seq'=64] {'batch','seq'}, dimensions={0} | all-to-all | bytes 1048576 | tf_op jit(solution)/shard_map/all_to_all | solution.py:227
  75.2 0.9 %finish.1 = (bf16[1,256,256]{2,1,0:T(8,128)(2,1)}, f32[256,256]{1,0:T(8,128)}) custom-call(f32[1024,128]{1,0:T(8,128)S(1)} %bitcast.16), custom_call_target="tpu_custom_call" | custom-call | tf_op jit(solution)/shard_map/finish/pallas_call | solution.py:195
  (3 shorter events, 0.1 us)
Async XLA Ops:
  0.6 1.0 %copy-start = (f32[256,256]{1,0:T(8,128)S(1)}, f32[256,256]{1,0:T(8,128)}, u32[]{:S(2)}) copy-start(f32[256,256]{1,0:T(8,128)} %param.6) | copy-start | bytes 786436
  0.6 1.0 %copy-start.1 = (bf16[1,256,256]{2,1,0:T(8,128)(2,1)S(1)}, bf16[1,256,256]{2,1,0:T(8,128)(2,1)}, u32[]{:S(2)}) copy-start(bf16[1,256,256]{2,1,0:T(8,128)(2,1)} %param.5) | copy-start | bytes 393220
  1.6 1.0 %copy-start.2 = (f32[256]{0:T(256)S(1)}, f32[256]{0:T(256)}, u32[]{:S(2)}) copy-start(f32[256]{0:T(256)} %param.7) | copy-start | bytes 3076

commit v4 on v3

--- a/solution.py
+++ b/solution.py
@@ -13,7 +13,7 @@
 HALVES = BLOCK // LANES
 PACK = 16
 SENT = 5
-BACK = 4
+BACK = 3
 
 
 def product(left, right):
@@ -141,10 +141,10 @@
     lax.fori_loop(0, batch - 1, step, 0)
     one_batch(batch - 1, True)
     for b in range(batch):
-        for half in range(HALVES):
-            out_ref[pl.ds(b * blocks * BACK + HALVES + half, blocks, stride=BACK), :] = total[
-                0, :, half * LANES : (half + 1) * LANES
-            ]
+        half = b % HALVES
+        out_ref[pl.ds(b * blocks * BACK + HALVES, blocks, stride=BACK), :] = total[
+            0, :, half * LANES : (half + 1) * LANES
+        ]
 
 
 def correlations(got, batch, blocks):
@@ -167,47 +167,87 @@
     )(got)
 
 
-def finish(home_ref, input_ref, filter_ref, own, shared, left):
-    channels = filter_ref.shape[1]
+def write_out(pairs, left):
+    copies = [
+        pltpu.make_async_copy(source, target, left.at[place])
+        for place, (source, target) in enumerate(pairs)
+    ]
+    for copy in copies:
+        copy.start()
+    return copies
+
+
+def turn(home_ref, half_ref):
+    channels = half_ref.shape[1]
+    half_ref[...] = home_ref[pl.ds(HALVES, channels, stride=BACK), :].T
+
+
+def filter_half(home):
+    channels = home.shape[0] // BACK
+    vmem = pl.BlockSpec(memory_space=pltpu.VMEM)
+    return pl.pallas_call(
+        turn,
+        out_shape=jax.ShapeDtypeStruct((LANES, channels), jnp.float32),
+        in_specs=[vmem],
+        out_specs=vmem,
+        compiler_params=pltpu.CompilerParams(vmem_limit_bytes=16 * 1024 * 1024),
+        name="turn",
+    )(home)
+
+
+def finish(home_ref, input_ref, own, left):
+    channels = input_ref.shape[2]
     copies = []
-
-    def send_home(source, target):
-        copies.append(pltpu.make_async_copy(source, target, left.at[len(copies)]))
-        copies[-1].start()
-
-    for half in range(HALVES):
-        rows = slice(half * LANES, (half + 1) * LANES)
-        shared[rows, :] = home_ref[pl.ds(HALVES + half, channels, stride=BACK), :].T
-        send_home(shared.at[rows, :], filter_ref.at[rows, :])
     for half in range(HALVES):
         rows = slice(half * LANES, (half + 1) * LANES)
         conv = home_ref[pl.ds(half, channels, stride=BACK), :].T
         own[0, rows, :] = conv.astype(jnp.bfloat16)
-        send_home(own.at[:, rows, :], input_ref.at[:, rows, :])
+        copies += write_out([(own.at[:, rows, :], input_ref.at[:, rows, :])], left.at[pl.ds(half, 1)])
     for copy in copies:
         copy.wait()
 
 
-def gradients(home):
+def input_gradient(home):
     channels = home.shape[0] // BACK
-    vmem = pl.BlockSpec(memory_space=pltpu.VMEM)
-    hbm = pl.BlockSpec(memory_space=pltpu.HBM)
     return pl.pallas_call(
         finish,
-        out_shape=(
-            jax.ShapeDtypeStruct((1, BLOCK, channels), jnp.bfloat16),
-            jax.ShapeDtypeStruct((BLOCK, channels), jnp.float32),
-        ),
-        in_specs=[vmem],
-        out_specs=(hbm, hbm),
+        out_shape=jax.ShapeDtypeStruct((1, BLOCK, channels), jnp.bfloat16),
+        in_specs=[pl.BlockSpec(memory_space=pltpu.VMEM)],
+        out_specs=pl.BlockSpec(memory_space=pltpu.HBM),
         scratch_shapes=[
             pltpu.VMEM((1, BLOCK, channels), jnp.bfloat16),
-            pltpu.VMEM((BLOCK, channels), jnp.float32),
-            pltpu.SemaphoreType.DMA((2 * HALVES,)),
+            pltpu.SemaphoreType.DMA((HALVES,)),
         ],
         compiler_params=pltpu.CompilerParams(vmem_limit_bytes=16 * 1024 * 1024),
+        cost_estimate=pl.CostEstimate(flops=1_000_000_000, bytes_accessed=1_000_000, transcendentals=0),
         name="finish",
     )(home)
+
+
+def join(own_ref, other_ref, filter_ref, left):
+    core = lax.rem(lax.axis_index("batch"), HALVES)
+    copies = write_out(
+        [
+            (own_ref, filter_ref.at[pl.ds(pl.multiple_of(core * LANES, LANES), LANES), :]),
+            (other_ref, filter_ref.at[pl.ds(pl.multiple_of((1 - core) * LANES, LANES), LANES), :]),
+        ],
+        left,
+    )
+    for copy in copies:
+        copy.wait()
+
+
+def filter_gradient(own, other):
+    vmem = pl.BlockSpec(memory_space=pltpu.VMEM)
+    return pl.pallas_call(
+        join,
+        out_shape=jax.ShapeDtypeStruct((BLOCK, own.shape[1]), jnp.float32),
+        in_specs=[vmem, vmem],
+        out_specs=pl.BlockSpec(memory_space=pltpu.HBM),
+        scratch_shapes=[pltpu.SemaphoreType.DMA((HALVES,))],
+        compiler_params=pltpu.CompilerParams(vmem_limit_bytes=16 * 1024 * 1024),
+        name="join",
+    )(own, other)
 
 
 def shards(signal, grad_out, filter_taps, skip_gain):
@@ -218,14 +258,18 @@
     grad_rows = grad_out[0].astype(jnp.float32)
     signal_rows = signal[0].astype(jnp.float32)
     gain = jnp.broadcast_to(skip_gain[:, None], (channels, LANES - per_batch))
+    signal_rows, grad_rows, gain = lax.optimization_barrier((signal_rows, grad_rows, gain))
     taps = lax.dynamic_slice_in_dim(filter_taps, lax.axis_index("batch") * per_batch, per_batch, 0)
     sent = jnp.concatenate(
         [signal_rows.T, grad_rows.T, taps.T, gain], axis=1
     ).reshape(channels, SENT, 1, LANES)
     got = lax.all_to_all(sent, axes, 0, 0, tiled=True)
     back = correlations(got.reshape(channels * SENT, LANES), batch, blocks)
-    home = lax.all_to_all(back.reshape(channels, BACK, LANES), axes, 0, 0, tiled=True)
-    return gradients(home.reshape(channels * BACK, LANES))
+    home = lax.all_to_all(back.reshape(channels, BACK, 1, LANES), axes, 0, 0, tiled=True)
+    home = home.reshape(channels * BACK, LANES)
+    own = filter_half(home)
+    other = lax.ppermute(own, "batch", [(b, b ^ 1) for b in range(batch)])
+    return (input_gradient(home), filter_gradient(own, other))
 
 
 def solution(mesh):

time: 76.2 us -> 74.2 us (0.974)
  blocking collectives: 64.4 us -> 61.7 us
  local copies, waits for them, and re-layouts: 1.44 us -> 0.5 us
    all_to_all x1, blocking collectives: 26.1 us -> 23.4 us  [shards(): lax.all_to_all(back.reshape(channels, BACK, 1, LANES), axes, 0, 0, tiled=...]
    convert_element_type x0 -> x1, other arithmetic: none -> 1.05 us  [shards(): grad_rows = grad_out[0].astype(jnp.float32)]
    transpose x1 -> x0, other arithmetic: 0.95 us -> none  [shards(): sent = jnp.concatenate([signal_rows.T, grad_rows.T, taps.T, gain], axis=1...]
    unnamed x6 -> x4, local copies, waits for them, and re-layouts: 0.97 us -> 0.01 us
    pallas_call x1 -> x3, Pallas kernels: 0.87 us -> 1.58 us  [the longest x1 0.77 us: input_gradient(): pl.pallas_call(finish, out_shape=jax.ShapeDtypeStruct((1, BLOCK, channels...]
  transfers between devices with their start and end apart: 0 -> 1, of which waited for: 0 -> 1; matrix products, arithmetic and copies ran while one was open for 0% -> 0% of each run, Pallas kernels for 0% -> 1%
where the time goes in v4:
time: 74.2 us; the launch traced here: 74.1 us
  blocking collectives  61.7 us (83%)
  Pallas kernels  9.23 us (12%)
  other arithmetic  1.1 us (1%)
    all_to_all x1, blocking collectives, shards(): got = lax.all_to_all(sent, axes, 0, 0, tiled=True)  38.3 us
    all_to_all x1, blocking collectives, shards(): lax.all_to_all(back.reshape(channels, BACK, 1, LANES), axes, 0, 0, tiled=...  23.4 us
    pallas_call x1, Pallas kernels, correlations(): pl.pallas_call(functools.partial(correlate, batch, blocks), out_shape=jax...  7.66 us
  transfers between devices with their start and end apart: 1, of which 1 were waited for; matrix products, arithmetic and copies ran while one was open for 0% of the time, Pallas kernels for 1%

profile of v4, /device:TPU:1, one launch (start us, length us, event | category | flops | bytes accessed | tf_op | source)
XLA Modules:
  0.0 74.1 jit_solution(2475042579775843183)
XLA Ops:
  0.6 0.0 copy-start
  0.7 0.0 copy-start.1
  0.7 1.1 %bitcast_convert_fusion = (f32[256,256]{1,0:T(8,128)S(1)}, f32[256,256]{1,0:T(8,128)S(1)}) fusion(bf16[1,256,256]{2,1,0:T(8,128)(2,1)} %param.5, bf16[1,256,256]{2,1,0:T(8,128)(2,1)} %param.4), kind=kLoop, calls=%fused_computation.1 | loop fusion | flops 131072 | bytes 786432 | tf_op jit(solution)/shard_map/convert_element_type | solution.py:258
  1.7 0.0 copy-done.1
  1.7 0.0 copy-done
  1.8 0.5 copy.10
  2.3 38.3 %all_to_all.10 = f32[256,5,1,128]{3,2,1,0:T(1,128)S(1)} all-to-all(f32[256,5,1,128]{3,2,1,0:T(1,128)S(1)} %copy.10), channel_id=1, replica_groups=mesh['batch'=4,'seq'=64] {'batch','seq'}, dimensions={0} | all-to-all | bytes 1310720 | tf_op jit(solution)/shard_map/all_to_all | solution.py:266
  40.6 7.7 %correlate.1 = f32[768,128]{1,0:T(8,128)S(1)} custom-call(f32[1280,128]{1,0:T(8,128)S(1)} %bitcast.16), custom_call_target="tpu_custom_call" | custom-call | flops 6000000000 | bytes 2000000 | tf_op jit(solution)/shard_map/correlate/pallas_call | solution.py:152
  48.3 23.4 %all_to_all.11 = f32[256,3,1,128]{3,2,1,0:T(1,128)S(1)} all-to-all(f32[256,3,1,128]{3,2,1,0:T(1,128)S(1)} %bitcast.17), channel_id=1, replica_groups=mesh['batch'=4,'seq'=64] {'batch','seq'}, dimensions={0} | all-to-all | bytes 786432 | tf_op jit(solution)/shard_map/all_to_all | solution.py:268
  71.6 0.1 turn.1.own_ref
  71.7 0.7 collective-permute-start
  72.4 0.8 %finish.1 = bf16[1,256,256]{2,1,0:T(8,128)(2,1)} custom-call(f32[768,128]{1,0:T(8,128)S(1)} %bitcast.15), custom_call_target="tpu_custom_call" | custom-call | flops 1000000000 | bytes 1000000 | tf_op jit(solution)/shard_map/finish/pallas_call | solution.py:212
  73.2 0.2 collective-permute-done.other_ref
  73.4 0.7 join.1
  (3 shorter events, 0.1 us)
Async XLA Ops:
  0.6 1.1 %copy-start = (f32[256,256]{1,0:T(8,128)S(1)}, f32[256,256]{1,0:T(8,128)}, u32[]{:S(2)}) copy-start(f32[256,256]{1,0:T(8,128)} %param.6) | copy-start | bytes 786436
  0.7 1.1 %copy-start.1 = (f32[256]{0:T(256)S(1)}, f32[256]{0:T(256)}, u32[]{:S(2)}) copy-start(f32[256]{0:T(256)} %param.7) | copy-start | bytes 3076
  71.7 1.7 %collective-permute-start = (f32[128,256]{1,0:T(8,128)S(1)}, f32[128,256]{1,0:T(8,128)S(1)}, u32[]{:S(2)}, u32[]{:S(2)}) collective-permute-start(f32[128,256]{1,0:T(8,128)S(1)} %turn.1.own_ref), channel_id=1, source_target_pairs={{0,64},{64,0},{128,192},{192,128},{1,65},{65,1},{129,193},{193,129... | collective-permute-start | bytes 393224 | tf_op jit(solution)/shard_map/ppermute | solution.py:271

commit v5 on v4

v5 whole, which is shorter than its diff:
```python
import functools

import jax
import jax.numpy as jnp
from jax import lax
from jax.experimental import pallas as pl
from jax.experimental.pallas import tpu as pltpu
from jax.sharding import PartitionSpec as P

LANES = 128
ROWS = 8
BLOCK = 256
HALVES = BLOCK // LANES
SENT = 5
BACK = 3


def product(left, right):
    return jnp.dot(left, right, preferred_element_type=jnp.float32)


def send(per_batch, signal_ref, grad_ref, taps_ref, gain_ref, sent_ref):
    channels = gain_ref.shape[1]
    for half in range(HALVES):
        rows = slice(half * LANES, (half + 1) * LANES)
        sent_ref[pl.ds(half, channels, stride=SENT), :] = signal_ref[rows, :].T
        sent_ref[pl.ds(HALVES + half, channels, stride=SENT), :] = grad_ref[rows, :].T
    first = pl.multiple_of(lax.axis_index("batch") * per_batch, per_batch)
    taps = taps_ref[pl.ds(first, per_batch), :]
    sent_ref[pl.ds(SENT - 1, channels, stride=SENT), :] = jnp.concatenate(
        [taps, gain_ref[...]], axis=0
    ).T


def pieces_to_send(signal_rows, grad_rows, filter_taps, gain, per_batch):
    channels = gain.shape[1]
    vmem = pl.BlockSpec(memory_space=pltpu.VMEM)
    return pl.pallas_call(
        functools.partial(send, per_batch),
        out_shape=jax.ShapeDtypeStruct((channels * SENT, LANES), jnp.float32),
        in_specs=[vmem] * 4,
        out_specs=vmem,
        compiler_params=pltpu.CompilerParams(vmem_limit_bytes=16 * 1024 * 1024),
        name="send",
    )(signal_rows, grad_rows, filter_taps, gain)


def correlate(batch, blocks, got_ref, out_ref, even, odd, ordered, total):
    turns = blocks // 2
    groups = turns // ROWS
    per_batch = BLOCK // batch
    window = LANES // 2
    gain = jnp.broadcast_to(got_ref[SENT - 1 : SENT, per_batch : per_batch + 1], (1, LANES))
    row = lax.broadcasted_iota(jnp.int32, (window, LANES), 0)
    lane = lax.broadcasted_iota(jnp.int32, (window, LANES), 1)
    own = lane <= 2 * row + 1
    nothing = jnp.zeros((window, LANES), jnp.float32)
    source = lax.broadcasted_iota(jnp.int32, (BLOCK, BLOCK), 0)
    target = lax.broadcasted_iota(jnp.int32, (BLOCK, BLOCK), 1)
    step = source // 2
    place = LANES * (source % 2) + window * (step // window) + (window - 1 - step % window)
    lanes_to = jnp.where(place == target, 1.0, 0.0).astype(jnp.bfloat16)
    target = lax.broadcasted_iota(jnp.int32, (blocks, blocks), 0)
    source = lax.broadcasted_iota(jnp.int32, (blocks, blocks), 1)
    place = turns * (source % 2) + (turns - 1 - source // 2)
    rows_to = jnp.where(place == target, 1.0, 0.0).astype(jnp.bfloat16)

    def rows_of(b, part):
        return got_ref[pl.ds(b * blocks * SENT + part, blocks, stride=SENT), :]

    def put_in_order(kind, halves):
        values = jnp.concatenate(halves, axis=1).astype(jnp.bfloat16)
        moved = product(rows_to, product(values, lanes_to).astype(jnp.bfloat16))
        for parity in range(2):
            for side in range(2):
                ordered[kind, parity, side, 0:turns, :] = moved[
                    side * turns : (side + 1) * turns, parity * LANES : (parity + 1) * LANES
                ]
                ordered[kind, parity, side, turns : turns + ROWS, :] = jnp.zeros(
                    (ROWS, LANES), jnp.float32
                )

    def turned(b, block):
        values = got_ref[pl.ds((b * blocks + block // 2) * SENT + HALVES + block % 2, 1), :]
        return pltpu.roll(jnp.broadcast_to(values, (window, LANES)), 2, 1, stride=2, stride_axis=0)

    def build(b, group, hankel):
        first = 4 * ROWS * group

        def at(block):
            return turned(b, block) if block < 2 * blocks else nothing

        current = at(first)
        for inner in range(4 * ROWS + 3):
            following = at(first + inner + 1)
            hankel[inner * window : (inner + 1) * window, :] = jnp.where(
                own, current, following
            ).astype(jnp.bfloat16)
            current = following

    def multiply(b, group, hankel):
        height = ROWS * (group + 1)
        base = turns - height
        result = None
        for inner in range(ROWS):
            start = base + ROWS - 1 - inner
            left = jnp.concatenate(
                [
                    jnp.concatenate(
                        [ordered[kind, parity, side, pl.ds(start, height), :] for side in range(2)],
                        axis=1,
                    )
                    for kind in (b, batch, batch + 1)
                    for parity in range(2)
                ],
                axis=0,
            ).astype(jnp.bfloat16)
            right = jnp.concatenate(
                [
                    hankel[(4 * inner + part) * window : (4 * inner + part) * window + BLOCK, :]
                    for part in range(4)
                ],
                axis=1,
            )
            term = product(left, right)
            result = term if result is None else result + term
        for parity in range(2):
            part = result[parity * height : (parity + 1) * height]
            high = result[(2 + parity) * height : (3 + parity) * height]
            low = result[(4 + parity) * height : (5 + parity) * height]
            for run in range(4):
                lanes = slice(run * LANES, (run + 1) * LANES)
                total[batch, parity, run, 0:height, :] += part[:, lanes]
                if group == 0:
                    total[b, parity, run, 0:height, :] = high[:, lanes] + low[:, lanes]
                    total[b, parity, run, height : turns + ROWS, :] = jnp.zeros(
                        (turns + ROWS - height, LANES), jnp.float32
                    )
                else:
                    total[b, parity, run, 0:height, :] += high[:, lanes] + low[:, lanes]

    build(0, 0, even)
    pieces = LANES // per_batch
    taps = [
        jnp.concatenate(
            [rows_of(half * pieces + piece, SENT - 1)[:, :per_batch] for piece in range(pieces)],
            axis=1,
        )
        for half in range(HALVES)
    ]
    high = [half.astype(jnp.bfloat16).astype(jnp.float32) for half in taps]
    put_in_order(batch, high)
    put_in_order(batch + 1, [half - part for half, part in zip(taps, high)])
    for b in range(batch):
        put_in_order(b, [rows_of(b, half) for half in range(HALVES)])
    total[batch] = jnp.zeros(total.shape[1:], jnp.float32)

    def one_batch(b, last):
        for group in range(groups):
            now, later = (even, odd) if group % 2 == 0 else (odd, even)
            if group + 1 < groups:
                build(b, group + 1, later)
            elif not last:
                build(b + 1, 0, later)
            multiply(b, group, now)

    def one_step(b, carry):
        one_batch(b, False)
        return carry

    lax.fori_loop(0, batch - 1, one_step, 0)
    one_batch(batch - 1, True)

    last_lane = lax.broadcasted_iota(jnp.int32, (turns, LANES), 1) == LANES - 1
    for kind in range(batch + 1):
        late = [pltpu.roll(total[kind, 1, run, 0:turns, :], LANES - 1, 1) for run in range(4)]
        late.append(pltpu.roll(total[kind, 1, 0, 1 : turns + 1, :], LANES - 1, 1))
        for run in range(4):
            side, half = run // 2, run % 2
            joined = total[kind, 0, run, 0:turns, :] + jnp.where(
                last_lane, late[run + 1], late[run]
            )
            if kind < batch:
                place = (kind * blocks + side) * SENT + HALVES + half
                joined = joined + gain * got_ref[pl.ds(place, turns, stride=2 * SENT), :]
                out_ref[pl.ds((kind * blocks + side) * BACK + half, turns, stride=2 * BACK), :] = joined
            else:
                for b in range(half, batch, HALVES):
                    place = (b * blocks + side) * BACK + HALVES
                    out_ref[pl.ds(place, turns, stride=2 * BACK), :] = joined


def correlations(got, batch, blocks):
    turns = blocks // 2
    hankel = pltpu.VMEM(((4 * ROWS + 3) * LANES // 2, LANES), jnp.bfloat16)
    return pl.pallas_call(
        functools.partial(correlate, batch, blocks),
        out_shape=jax.ShapeDtypeStruct((batch * blocks * BACK, LANES), jnp.float32),
        in_specs=[pl.BlockSpec(memory_space=pltpu.VMEM)],
        out_specs=pl.BlockSpec(memory_space=pltpu.VMEM),
        scratch_shapes=[
            hankel,
            hankel,
            pltpu.VMEM((batch + 2, 2, 2, turns + ROWS, LANES), jnp.float32),
            pltpu.VMEM((batch + 1, 2, 4, turns + ROWS, LANES), jnp.float32),
        ],
        compiler_params=pltpu.CompilerParams(vmem_limit_bytes=24 * 1024 * 1024),
        cost_estimate=pl.CostEstimate(flops=6_000_000_000, bytes_accessed=2_000_000, transcendentals=0),
        name="correlate",
    )(got)


def write_out(pairs, left):
    copies = [
        pltpu.make_async_copy(source, target, left.at[place])
        for place, (source, target) in enumerate(pairs)
    ]
    for copy in copies:
        copy.start()
    return copies


def turn(home_ref, half_ref):
    channels = half_ref.shape[1]
    half_ref[...] = home_ref[pl.ds(HALVES, channels, stride=BACK), :].T


def filter_half(home):
    channels = home.shape[0] // BACK
    vmem = pl.BlockSpec(memory_space=pltpu.VMEM)
    return pl.pallas_call(
        turn,
        out_shape=jax.ShapeDtypeStruct((LANES, channels), jnp.float32),
        in_specs=[vmem],
        out_specs=vmem,
        compiler_params=pltpu.CompilerParams(vmem_limit_bytes=16 * 1024 * 1024),
        name="turn",
    )(home)


def finish(home_ref, input_ref, own, left):
    channels = input_ref.shape[2]
    copies = []
    for half in range(HALVES):
        rows = slice(half * LANES, (half + 1) * LANES)
        conv = home_ref[pl.ds(half, channels, stride=BACK), :].T
        own[0, rows, :] = conv.astype(jnp.bfloat16)
        copies += write_out([(own.at[:, rows, :], input_ref.at[:, rows, :])], left.at[pl.ds(half, 1)])
    for copy in copies:
        copy.wait()


def input_gradient(home):
    channels = home.shape[0] // BACK
    return pl.pallas_call(
        finish,
        out_shape=jax.ShapeDtypeStruct((1, BLOCK, channels), jnp.bfloat16),
        in_specs=[pl.BlockSpec(memory_space=pltpu.VMEM)],
        out_specs=pl.BlockSpec(memory_space=pltpu.HBM),
        scratch_shapes=[
            pltpu.VMEM((1, BLOCK, channels), jnp.bfloat16),
            pltpu.SemaphoreType.DMA((HALVES,)),
        ],
        compiler_params=pltpu.CompilerParams(vmem_limit_bytes=16 * 1024 * 1024),
        cost_estimate=pl.CostEstimate(flops=1_000_000_000, bytes_accessed=1_000_000, transcendentals=0),
        name="finish",
    )(home)


def join(own_ref, other_ref, filter_ref, left):
    core = lax.rem(lax.axis_index("batch"), HALVES)
    copies = write_out(
        [
            (own_ref, filter_ref.at[pl.ds(pl.multiple_of(core * LANES, LANES), LANES), :]),
            (other_ref, filter_ref.at[pl.ds(pl.multiple_of((1 - core) * LANES, LANES), LANES), :]),
        ],
        left,
    )
    for copy in copies:
        copy.wait()


def filter_gradient(own, other):
    vmem = pl.BlockSpec(memory_space=pltpu.VMEM)
    return pl.pallas_call(
        join,
        out_shape=jax.ShapeDtypeStruct((BLOCK, own.shape[1]), jnp.float32),
        in_specs=[vmem, vmem],
        out_specs=pl.BlockSpec(memory_space=pltpu.HBM),
        scratch_shapes=[pltpu.SemaphoreType.DMA((HALVES,))],
        compiler_params=pltpu.CompilerParams(vmem_limit_bytes=16 * 1024 * 1024),
        name="join",
    )(own, other)


def shards(signal, grad_out, filter_taps, skip_gain):
    batch, blocks = lax.axis_size("batch"), lax.axis_size("seq")
    axes = ("batch", "seq")
    channels = filter_taps.shape[1]
    grad_rows = grad_out[0].astype(jnp.float32)
    signal_rows = signal[0].astype(jnp.float32)
    per_batch = BLOCK // batch
    gain = jnp.broadcast_to(skip_gain[None, :], (LANES - per_batch, channels))
    signal_rows, grad_rows, gain = lax.optimization_barrier((signal_rows, grad_rows, gain))
    sent = pieces_to_send(signal_rows, grad_rows, filter_taps, gain, per_batch)
    sent = sent.reshape(channels, SENT, 1, LANES)
    got = lax.all_to_all(sent, axes, 0, 0, tiled=True)
    back = correlations(got.reshape(channels * SENT, LANES), batch, blocks)
    home = lax.all_to_all(back.reshape(channels, BACK, 1, LANES), axes, 0, 0, tiled=True)
    home = home.reshape(channels * BACK, LANES)
    own = filter_half(home)
    other = lax.ppermute(own, "batch", [(b, b ^ 1) for b in range(batch)])
    return (input_gradient(home), filter_gradient(own, other))


def solution(mesh):
    return jax.shard_map(
        shards,
        mesh=mesh,
        in_specs=(P("batch", "seq", None), P("batch", "seq", None), P("seq", None), P()),
        out_specs=(P("batch", "seq", None), P("seq", None)),
        check_vma=False,
    )
```

time: 74.2 us -> 73.7 us (level)
  no operation moved by 1% of the time
where the time goes in v5:
time: 73.7 us; the launch traced here: 73.5 us
  blocking collectives  61.7 us (84%)
  Pallas kernels  9.24 us (13%)
  other arithmetic  1.05 us (1%)
    all_to_all x1, blocking collectives, shards(): got = lax.all_to_all(sent, axes, 0, 0, tiled=True)  38.3 us
    all_to_all x1, blocking collectives, shards(): lax.all_to_all(back.reshape(channels, BACK, 1, LANES), axes, 0, 0, tiled=...  23.4 us
    pallas_call x1, Pallas kernels, correlations(): pl.pallas_call(functools.partial(correlate, batch, blocks), out_shape=jax...  7.44 us
  transfers between devices with their start and end apart: 1, of which 1 were waited for; matrix products, arithmetic and copies ran while one was open for 0% of the time, Pallas kernels for 1%

profile of v5, /device:TPU:1, one launch (start us, length us, event | category | flops | bytes accessed | tf_op | source)
XLA Modules:
  0.0 73.5 jit_solution(11353477687501513658)
XLA Ops:
  0.6 0.0 copy-start.1
  0.6 0.0 copy-start
  0.7 1.0 %bitcast_convert_fusion = (f32[256,256]{1,0:T(8,128)S(1)}, f32[256,256]{1,0:T(8,128)S(1)}) fusion(bf16[1,256,256]{2,1,0:T(8,128)(2,1)} %param.5, bf16[1,256,256]{2,1,0:T(8,128)(2,1)} %param.4), kind=kLoop, calls=%fused_computation | loop fusion | flops 131072 | bytes 786432 | tf_op jit(solution)/shard_map/convert_element_type | solution.py:300
  1.7 0.0 copy-done.1
  1.7 0.0 copy-done
  1.7 0.2 send.1
  2.0 38.3 %all_to_all.10 = f32[256,5,1,128]{3,2,1,0:T(1,128)S(1)} all-to-all(f32[256,5,1,128]{3,2,1,0:T(1,128)S(1)} %bitcast.10), channel_id=1, replica_groups=mesh['batch'=4,'seq'=64] {'batch','seq'}, dimensions={0} | all-to-all | bytes 1310720 | tf_op jit(solution)/shard_map/all_to_all | solution.py:307
  40.3 7.4 %correlate.1 = f32[768,128]{1,0:T(8,128)S(1)} custom-call(f32[1280,128]{1,0:T(8,128)S(1)} %bitcast.13), custom_call_target="tpu_custom_call" | custom-call | flops 6000000000 | bytes 2000000 | tf_op jit(solution)/shard_map/correlate/pallas_call | solution.py:196
  47.7 23.4 %all_to_all.11 = f32[256,3,1,128]{3,2,1,0:T(1,128)S(1)} all-to-all(f32[256,3,1,128]{3,2,1,0:T(1,128)S(1)} %bitcast.14), channel_id=1, replica_groups=mesh['batch'=4,'seq'=64] {'batch','seq'}, dimensions={0} | all-to-all | bytes 786432 | tf_op jit(solution)/shard_map/all_to_all | solution.py:309
  71.1 0.1 turn.1.own_ref
  71.2 0.7 collective-permute-start
  71.8 0.8 %finish.1 = bf16[1,256,256]{2,1,0:T(8,128)(2,1)} custom-call(f32[768,128]{1,0:T(8,128)S(1)} %bitcast.12), custom_call_target="tpu_custom_call" | custom-call | flops 1000000000 | bytes 1000000 | tf_op jit(solution)/shard_map/finish/pallas_call | solution.py:255
  72.6 0.2 collective-permute-done.other_ref
  72.8 0.7 join.1
  (1 shorter events, 0.0 us)
Async XLA Ops:
  0.6 1.1 %copy-start.1 = (f32[256]{0:T(256)S(1)}, f32[256]{0:T(256)}, u32[]{:S(2)}) copy-start(f32[256]{0:T(256)} %param.7) | copy-start | bytes 3076
  0.6 1.1 %copy-start = (f32[256,256]{1,0:T(8,128)S(1)}, f32[256,256]{1,0:T(8,128)}, u32[]{:S(2)}) copy-start(f32[256,256]{1,0:T(8,128)} %taps_ref.1) | copy-start | bytes 786436
  71.2 1.7 %collective-permute-start = (f32[128,256]{1,0:T(8,128)S(1)}, f32[128,256]{1,0:T(8,128)S(1)}, u32[]{:S(2)}, u32[]{:S(2)}) collective-permute-start(f32[128,256]{1,0:T(8,128)S(1)} %turn.1.own_ref), channel_id=1, source_target_pairs={{0,64},{64,0},{128,192},{192,128},{1,65},{65,1},{129,193},{193,129... | collective-permute-start | bytes 393224 | tf_op jit(solution)/shard_map/ppermute | solution.py:312

commit v6 on v5

--- a/solution.py
+++ b/solution.py
@@ -11,6 +11,7 @@
 ROWS = 8
 BLOCK = 256
 HALVES = BLOCK // LANES
+PACK = 16
 SENT = 5
 BACK = 3
 
@@ -46,8 +47,7 @@
 
 
 def correlate(batch, blocks, got_ref, out_ref, even, odd, ordered, total):
-    turns = blocks // 2
-    groups = turns // ROWS
+    groups = blocks // PACK
     per_batch = BLOCK // batch
     window = LANES // 2
     gain = jnp.broadcast_to(got_ref[SENT - 1 : SENT, per_batch : per_batch + 1], (1, LANES))
@@ -62,8 +62,7 @@
     lanes_to = jnp.where(place == target, 1.0, 0.0).astype(jnp.bfloat16)
     target = lax.broadcasted_iota(jnp.int32, (blocks, blocks), 0)
     source = lax.broadcasted_iota(jnp.int32, (blocks, blocks), 1)
-    place = turns * (source % 2) + (turns - 1 - source // 2)
-    rows_to = jnp.where(place == target, 1.0, 0.0).astype(jnp.bfloat16)
+    rows_to = jnp.where(source + target == blocks - 1, 1.0, 0.0).astype(jnp.bfloat16)
 
     def rows_of(b, part):
         return got_ref[pl.ds(b * blocks * SENT + part, blocks, stride=SENT), :]
@@ -72,26 +71,21 @@
         values = jnp.concatenate(halves, axis=1).astype(jnp.bfloat16)
         moved = product(rows_to, product(values, lanes_to).astype(jnp.bfloat16))
         for parity in range(2):
-            for side in range(2):
-                ordered[kind, parity, side, 0:turns, :] = moved[
-                    side * turns : (side + 1) * turns, parity * LANES : (parity + 1) * LANES
-                ]
-                ordered[kind, parity, side, turns : turns + ROWS, :] = jnp.zeros(
-                    (ROWS, LANES), jnp.float32
-                )
+            ordered[kind, parity, 0:blocks, :] = moved[:, parity * LANES : (parity + 1) * LANES]
+            ordered[kind, parity, blocks : blocks + PACK, :] = jnp.zeros((PACK, LANES), jnp.float32)
 
     def turned(b, block):
         values = got_ref[pl.ds((b * blocks + block // 2) * SENT + HALVES + block % 2, 1), :]
         return pltpu.roll(jnp.broadcast_to(values, (window, LANES)), 2, 1, stride=2, stride_axis=0)
 
     def build(b, group, hankel):
-        first = 4 * ROWS * group
+        first = 2 * PACK * group
 
         def at(block):
             return turned(b, block) if block < 2 * blocks else nothing
 
         current = at(first)
-        for inner in range(4 * ROWS + 3):
+        for inner in range(2 * PACK + 3):
             following = at(first + inner + 1)
             hankel[inner * window : (inner + 1) * window, :] = jnp.where(
                 own, current, following
@@ -99,15 +93,18 @@
             current = following
 
     def multiply(b, group, hankel):
-        height = ROWS * (group + 1)
-        base = turns - height
+        height = PACK * (group + 1)
+        base = blocks - height
         result = None
-        for inner in range(ROWS):
-            start = base + ROWS - 1 - inner
+        for inner in range(PACK // 2):
+            start = base + PACK - 1 - 2 * inner
             left = jnp.concatenate(
                 [
                     jnp.concatenate(
-                        [ordered[kind, parity, side, pl.ds(start, height), :] for side in range(2)],
+                        [
+                            ordered[kind, parity, pl.ds(start - later, height), :]
+                            for later in range(2)
+                        ],
                         axis=1,
                     )
                     for kind in (b, batch, batch + 1)
@@ -117,8 +114,8 @@
             ).astype(jnp.bfloat16)
             right = jnp.concatenate(
                 [
-                    hankel[(4 * inner + part) * window : (4 * inner + part) * window + BLOCK, :]
-                    for part in range(4)
+                    hankel[(4 * inner + half) * window : (4 * inner + half) * window + BLOCK, :]
+                    for half in range(HALVES)
                 ],
                 axis=1,
             )
@@ -128,16 +125,16 @@
             part = result[parity * height : (parity + 1) * height]
             high = result[(2 + parity) * height : (3 + parity) * height]
             low = result[(4 + parity) * height : (5 + parity) * height]
-            for run in range(4):
-                lanes = slice(run * LANES, (run + 1) * LANES)
-                total[batch, parity, run, 0:height, :] += part[:, lanes]
+            for half in range(HALVES):
+                lanes = slice(half * LANES, (half + 1) * LANES)
+                total[batch, parity, half, 0:height, :] += part[:, lanes]
                 if group == 0:
-                    total[b, parity, run, 0:height, :] = high[:, lanes] + low[:, lanes]
-                    total[b, parity, run, height : turns + ROWS, :] = jnp.zeros(
-                        (turns + ROWS - height, LANES), jnp.float32
+                    total[b, parity, half, 0:height, :] = high[:, lanes] + low[:, lanes]
+                    total[b, parity, half, height : blocks + ROWS, :] = jnp.zeros(
+                        (blocks + ROWS - height, LANES), jnp.float32
                     )
                 else:
-                    total[b, parity, run, 0:height, :] += high[:, lanes] + low[:, lanes]
+                    total[b, parity, half, 0:height, :] += high[:, lanes] + low[:, lanes]
 
     build(0, 0, even)
     pieces = LANES // per_batch
@@ -171,28 +168,24 @@
     lax.fori_loop(0, batch - 1, one_step, 0)
     one_batch(batch - 1, True)
 
-    last_lane = lax.broadcasted_iota(jnp.int32, (turns, LANES), 1) == LANES - 1
+    last_lane = lax.broadcasted_iota(jnp.int32, (blocks, LANES), 1) == LANES - 1
     for kind in range(batch + 1):
-        late = [pltpu.roll(total[kind, 1, run, 0:turns, :], LANES - 1, 1) for run in range(4)]
-        late.append(pltpu.roll(total[kind, 1, 0, 1 : turns + 1, :], LANES - 1, 1))
-        for run in range(4):
-            side, half = run // 2, run % 2
-            joined = total[kind, 0, run, 0:turns, :] + jnp.where(
-                last_lane, late[run + 1], late[run]
+        late = [pltpu.roll(total[kind, 1, half, 0:blocks, :], LANES - 1, 1) for half in range(HALVES)]
+        late.append(pltpu.roll(total[kind, 1, 0, 1 : blocks + 1, :], LANES - 1, 1))
+        for half in range(HALVES):
+            joined = total[kind, 0, half, 0:blocks, :] + jnp.where(
+                last_lane, late[half + 1], late[half]
             )
             if kind < batch:
-                place = (kind * blocks + side) * SENT + HALVES + half
-                joined = joined + gain * got_ref[pl.ds(place, turns, stride=2 * SENT), :]
-                out_ref[pl.ds((kind * blocks + side) * BACK + half, turns, stride=2 * BACK), :] = joined
+                joined = joined + gain * rows_of(kind, HALVES + half)
+                out_ref[pl.ds(kind * blocks * BACK + half, blocks, stride=BACK), :] = joined
             else:
                 for b in range(half, batch, HALVES):
-                    place = (b * blocks + side) * BACK + HALVES
-                    out_ref[pl.ds(place, turns, stride=2 * BACK), :] = joined
+                    out_ref[pl.ds(b * blocks * BACK + HALVES, blocks, stride=BACK), :] = joined
 
 
 def correlations(got, batch, blocks):
-    turns = blocks // 2
-    hankel = pltpu.VMEM(((4 * ROWS + 3) * LANES // 2, LANES), jnp.bfloat16)
+    hankel = pltpu.VMEM(((2 * PACK + 3) * LANES // 2, LANES), jnp.bfloat16)
     return pl.pallas_call(
         functools.partial(correlate, batch, blocks),
         out_shape=jax.ShapeDtypeStruct((batch * blocks * BACK, LANES), jnp.float32),
@@ -201,8 +194,8 @@
         scratch_shapes=[
             hankel,
             hankel,
-            pltpu.VMEM((batch + 2, 2, 2, turns + ROWS, LANES), jnp.float32),
-            pltpu.VMEM((batch + 1, 2, 4, turns + ROWS, LANES), jnp.float32),
+            pltpu.VMEM((batch + 2, 2, blocks + PACK, LANES), jnp.float32),
+            pltpu.VMEM((batch + 1, 2, HALVES, blocks + ROWS, LANES), jnp.float32),
         ],
         compiler_params=pltpu.CompilerParams(vmem_limit_bytes=24 * 1024 * 1024),
         cost_estimate=pl.CostEstimate(flops=6_000_000_000, bytes_accessed=2_000_000, transcendentals=0),

time: 73.7 us -> 72.7 us (0.986)
  Pallas kernels: 9.24 us -> 8.23 us
    pallas_call x1, Pallas kernels: 7.44 us -> 6.43 us  [correlations(): pl.pallas_call(functools.partial(correlate, batch, blocks), out_shape=jax...]
where the time goes in v6:
time: 72.7 us; the launch traced here: 72.5 us
  blocking collectives  61.7 us (85%)
  Pallas kernels  8.23 us (11%)
  other arithmetic  1.05 us (1%)
    all_to_all x1, blocking collectives, shards(): got = lax.all_to_all(sent, axes, 0, 0, tiled=True)  38.3 us
    all_to_all x1, blocking collectives, shards(): lax.all_to_all(back.reshape(channels, BACK, 1, LANES), axes, 0, 0, tiled=...  23.4 us
    pallas_call x1, Pallas kernels, correlations(): pl.pallas_call(functools.partial(correlate, batch, blocks), out_shape=jax...  6.43 us
  transfers between devices with their start and end apart: 1, of which 1 were waited for; matrix products, arithmetic and copies ran while one was open for 0% of the time, Pallas kernels for 1%

profile of v6, /device:TPU:1, one launch (start us, length us, event | category | flops | bytes accessed | tf_op | source)
XLA Modules:
  0.0 72.5 jit_solution(11358534038076076511)
XLA Ops:
  0.6 0.0 copy-start.1
  0.6 0.0 copy-start
  0.7 1.0 %bitcast_convert_fusion = (f32[256,256]{1,0:T(8,128)S(1)}, f32[256,256]{1,0:T(8,128)S(1)}) fusion(bf16[1,256,256]{2,1,0:T(8,128)(2,1)} %param.5, bf16[1,256,256]{2,1,0:T(8,128)(2,1)} %param.4), kind=kLoop, calls=%fused_computation | loop fusion | flops 131072 | bytes 786432 | tf_op jit(solution)/shard_map/convert_element_type | solution.py:293
  1.7 0.0 copy-done.1
  1.7 0.0 copy-done
  1.7 0.2 send.1
  2.0 38.3 %all_to_all.10 = f32[256,5,1,128]{3,2,1,0:T(1,128)S(1)} all-to-all(f32[256,5,1,128]{3,2,1,0:T(1,128)S(1)} %bitcast.10), channel_id=1, replica_groups=mesh['batch'=4,'seq'=64] {'batch','seq'}, dimensions={0} | all-to-all | bytes 1310720 | tf_op jit(solution)/shard_map/all_to_all | solution.py:300
  40.3 6.4 %correlate.1 = f32[768,128]{1,0:T(8,128)S(1)} custom-call(f32[1280,128]{1,0:T(8,128)S(1)} %bitcast.13), custom_call_target="tpu_custom_call" | custom-call | flops 6000000000 | bytes 2000000 | tf_op jit(solution)/shard_map/correlate/pallas_call | solution.py:189
  46.7 23.4 %all_to_all.11 = f32[256,3,1,128]{3,2,1,0:T(1,128)S(1)} all-to-all(f32[256,3,1,128]{3,2,1,0:T(1,128)S(1)} %bitcast.14), channel_id=1, replica_groups=mesh['batch'=4,'seq'=64] {'batch','seq'}, dimensions={0} | all-to-all | bytes 786432 | tf_op jit(solution)/shard_map/all_to_all | solution.py:302
  70.1 0.1 turn.1.own_ref
  70.2 0.7 collective-permute-start
  70.8 0.8 %finish.1 = bf16[1,256,256]{2,1,0:T(8,128)(2,1)} custom-call(f32[768,128]{1,0:T(8,128)S(1)} %bitcast.12), custom_call_target="tpu_custom_call" | custom-call | flops 1000000000 | bytes 1000000 | tf_op jit(solution)/shard_map/finish/pallas_call | solution.py:248
  71.6 0.2 collective-permute-done.other_ref
  71.8 0.7 join.1
  (1 shorter events, 0.0 us)
Async XLA Ops:
  0.6 1.1 %copy-start.1 = (f32[256]{0:T(256)S(1)}, f32[256]{0:T(256)}, u32[]{:S(2)}) copy-start(f32[256]{0:T(256)} %param.7) | copy-start | bytes 3076
  0.6 1.1 %copy-start = (f32[256,256]{1,0:T(8,128)S(1)}, f32[256,256]{1,0:T(8,128)}, u32[]{:S(2)}) copy-start(f32[256,256]{1,0:T(8,128)} %taps_ref.1) | copy-start | bytes 786436
  70.2 1.7 %collective-permute-start = (f32[128,256]{1,0:T(8,128)S(1)}, f32[128,256]{1,0:T(8,128)S(1)}, u32[]{:S(2)}, u32[]{:S(2)}) collective-permute-start(f32[128,256]{1,0:T(8,128)S(1)} %turn.1.own_ref), channel_id=1, source_target_pairs={{0,64},{64,0},{128,192},{192,128},{1,65},{65,1},{129,193},{193,129... | collective-permute-start | bytes 393224 | tf_op jit(solution)/shard_map/ppermute | solution.py:305

commit v7 on v6

--- a/solution.py
+++ b/solution.py
@@ -92,12 +92,11 @@
             ).astype(jnp.bfloat16)
             current = following
 
-    def multiply(b, group, hankel):
-        height = PACK * (group + 1)
-        base = blocks - height
+    def multiply(b, group, part, hankel):
+        height = PACK * group + ROWS * (part + 1)
         result = None
-        for inner in range(PACK // 2):
-            start = base + PACK - 1 - 2 * inner
+        for inner in range(part * ROWS // 2, (part + 1) * ROWS // 2):
+            start = blocks - 1 - PACK * group - 2 * inner
             left = jnp.concatenate(
                 [
                     jnp.concatenate(
@@ -122,13 +121,13 @@
             term = product(left, right)
             result = term if result is None else result + term
         for parity in range(2):
-            part = result[parity * height : (parity + 1) * height]
+            shared = result[parity * height : (parity + 1) * height]
             high = result[(2 + parity) * height : (3 + parity) * height]
             low = result[(4 + parity) * height : (5 + parity) * height]
             for half in range(HALVES):
                 lanes = slice(half * LANES, (half + 1) * LANES)
-                total[batch, parity, half, 0:height, :] += part[:, lanes]
-                if group == 0:
+                total[batch, parity, half, 0:height, :] += shared[:, lanes]
+                if group == 0 and part == 0:
                     total[b, parity, half, 0:height, :] = high[:, lanes] + low[:, lanes]
                     total[b, parity, half, height : blocks + ROWS, :] = jnp.zeros(
                         (blocks + ROWS - height, LANES), jnp.float32
@@ -159,7 +158,8 @@
                 build(b, group + 1, later)
             elif not last:
                 build(b + 1, 0, later)
-            multiply(b, group, now)
+            for part in range(PACK // ROWS):
+                multiply(b, group, part, now)
 
     def one_step(b, carry):
         one_batch(b, False)

time: 72.7 us -> 72.3 us (level)
  no operation moved by 1% of the time
where the time goes in v7:
time: 72.3 us; the launch traced here: 72.1 us
  blocking collectives  61.7 us (85%)
  Pallas kernels  7.81 us (11%)
  other arithmetic  1.05 us (1%)
    all_to_all x1, blocking collectives, shards(): got = lax.all_to_all(sent, axes, 0, 0, tiled=True)  38.3 us
    all_to_all x1, blocking collectives, shards(): lax.all_to_all(back.reshape(channels, BACK, 1, LANES), axes, 0, 0, tiled=...  23.4 us
    pallas_call x1, Pallas kernels, correlations(): pl.pallas_call(functools.partial(correlate, batch, blocks), out_shape=jax...  6.01 us
  transfers between devices with their start and end apart: 1, of which 1 were waited for; matrix products, arithmetic and copies ran while one was open for 0% of the time, Pallas kernels for 1%

profile of v7, /device:TPU:1, one launch (start us, length us, event | category | flops | bytes accessed | tf_op | source)
XLA Modules:
  0.0 72.1 jit_solution(7112772637237606312)
XLA Ops:
  0.6 0.0 copy-start.1
  0.6 0.0 copy-start
  0.7 1.0 %bitcast_convert_fusion = (f32[256,256]{1,0:T(8,128)S(1)}, f32[256,256]{1,0:T(8,128)S(1)}) fusion(bf16[1,256,256]{2,1,0:T(8,128)(2,1)} %param.5, bf16[1,256,256]{2,1,0:T(8,128)(2,1)} %param.4), kind=kLoop, calls=%fused_computation | loop fusion | flops 131072 | bytes 786432 | tf_op jit(solution)/shard_map/convert_element_type | solution.py:293
  1.7 0.0 copy-done.1
  1.7 0.0 copy-done
  1.7 0.2 send.1
  2.0 38.3 %all_to_all.10 = f32[256,5,1,128]{3,2,1,0:T(1,128)S(1)} all-to-all(f32[256,5,1,128]{3,2,1,0:T(1,128)S(1)} %bitcast.10), channel_id=1, replica_groups=mesh['batch'=4,'seq'=64] {'batch','seq'}, dimensions={0} | all-to-all | bytes 1310720 | tf_op jit(solution)/shard_map/all_to_all | solution.py:300
  40.3 6.0 %correlate.1 = f32[768,128]{1,0:T(8,128)S(1)} custom-call(f32[1280,128]{1,0:T(8,128)S(1)} %bitcast.13), custom_call_target="tpu_custom_call" | custom-call | flops 6000000000 | bytes 2000000 | tf_op jit(solution)/shard_map/correlate/pallas_call | solution.py:189
  46.3 23.4 %all_to_all.11 = f32[256,3,1,128]{3,2,1,0:T(1,128)S(1)} all-to-all(f32[256,3,1,128]{3,2,1,0:T(1,128)S(1)} %bitcast.14), channel_id=1, replica_groups=mesh['batch'=4,'seq'=64] {'batch','seq'}, dimensions={0} | all-to-all | bytes 786432 | tf_op jit(solution)/shard_map/all_to_all | solution.py:302
  69.6 0.1 turn.1.own_ref
  69.7 0.7 collective-permute-start
  70.4 0.8 %finish.1 = bf16[1,256,256]{2,1,0:T(8,128)(2,1)} custom-call(f32[768,128]{1,0:T(8,128)S(1)} %bitcast.12), custom_call_target="tpu_custom_call" | custom-call | flops 1000000000 | bytes 1000000 | tf_op jit(solution)/shard_map/finish/pallas_call | solution.py:248
  71.2 0.2 collective-permute-done.other_ref
  71.4 0.7 join.1
  (1 shorter events, 0.0 us)
Async XLA Ops:
  0.6 1.1 %copy-start.1 = (f32[256]{0:T(256)S(1)}, f32[256]{0:T(256)}, u32[]{:S(2)}) copy-start(f32[256]{0:T(256)} %param.7) | copy-start | bytes 3076
  0.6 1.1 %copy-start = (f32[256,256]{1,0:T(8,128)S(1)}, f32[256,256]{1,0:T(8,128)}, u32[]{:S(2)}) copy-start(f32[256,256]{1,0:T(8,128)} %taps_ref.1) | copy-start | bytes 786436
  69.7 1.7 %collective-permute-start = (f32[128,256]{1,0:T(8,128)S(1)}, f32[128,256]{1,0:T(8,128)S(1)}, u32[]{:S(2)}, u32[]{:S(2)}) collective-permute-start(f32[128,256]{1,0:T(8,128)S(1)} %turn.1.own_ref), channel_id=1, source_target_pairs={{0,64},{64,0},{128,192},{192,128},{1,65},{65,1},{129,193},{193,129... | collective-permute-start | bytes 393224 | tf_op jit(solution)/shard_map/ppermute | solution.py:305

commit v8 on v7

--- a/solution.py
+++ b/solution.py
@@ -161,12 +161,8 @@
             for part in range(PACK // ROWS):
                 multiply(b, group, part, now)
 
-    def one_step(b, carry):
-        one_batch(b, False)
-        return carry
-
-    lax.fori_loop(0, batch - 1, one_step, 0)
-    one_batch(batch - 1, True)
+    for b in range(batch):
+        one_batch(b, b == batch - 1)
 
     last_lane = lax.broadcasted_iota(jnp.int32, (blocks, LANES), 1) == LANES - 1
     for kind in range(batch + 1):

time: 72.3 us -> 71.7 us (level)
  no operation moved by 1% of the time
where the time goes in v8:
time: 71.7 us; the launch traced here: 71.5 us
  blocking collectives  61.7 us (86%)
  Pallas kernels  7.24 us (10%)
  other arithmetic  1.05 us (1%)
    all_to_all x1, blocking collectives, shards(): got = lax.all_to_all(sent, axes, 0, 0, tiled=True)  38.3 us
    all_to_all x1, blocking collectives, shards(): lax.all_to_all(back.reshape(channels, BACK, 1, LANES), axes, 0, 0, tiled=...  23.4 us
    pallas_call x1, Pallas kernels, correlations(): pl.pallas_call(functools.partial(correlate, batch, blocks), out_shape=jax...  5.44 us
  transfers between devices with their start and end apart: 1, of which 1 were waited for; matrix products, arithmetic and copies ran while one was open for 0% of the time, Pallas kernels for 1%

profile of v8, /device:TPU:1, one launch (start us, length us, event | category | flops | bytes accessed | tf_op | source)
XLA Modules:
  0.0 71.5 jit_solution(7792183070425656113)
XLA Ops:
  0.6 0.0 copy-start.1
  0.6 0.0 copy-start
  0.7 1.0 %bitcast_convert_fusion = (f32[256,256]{1,0:T(8,128)S(1)}, f32[256,256]{1,0:T(8,128)S(1)}) fusion(bf16[1,256,256]{2,1,0:T(8,128)(2,1)} %param.5, bf16[1,256,256]{2,1,0:T(8,128)(2,1)} %param.4), kind=kLoop, calls=%fused_computation | loop fusion | flops 131072 | bytes 786432 | tf_op jit(solution)/shard_map/convert_element_type | solution.py:289
  1.7 0.0 copy-done.1
  1.7 0.0 copy-done
  1.7 0.2 send.1
  2.0 38.3 %all_to_all.10 = f32[256,5,1,128]{3,2,1,0:T(1,128)S(1)} all-to-all(f32[256,5,1,128]{3,2,1,0:T(1,128)S(1)} %bitcast.10), channel_id=1, replica_groups=mesh['batch'=4,'seq'=64] {'batch','seq'}, dimensions={0} | all-to-all | bytes 1310720 | tf_op jit(solution)/shard_map/all_to_all | solution.py:296
  40.3 5.4 %correlate.1 = f32[768,128]{1,0:T(8,128)S(1)} custom-call(f32[1280,128]{1,0:T(8,128)S(1)} %bitcast.13), custom_call_target="tpu_custom_call" | custom-call | flops 6000000000 | bytes 2000000 | tf_op jit(solution)/shard_map/correlate/pallas_call | solution.py:185
  45.7 23.4 %all_to_all.11 = f32[256,3,1,128]{3,2,1,0:T(1,128)S(1)} all-to-all(f32[256,3,1,128]{3,2,1,0:T(1,128)S(1)} %bitcast.14), channel_id=1, replica_groups=mesh['batch'=4,'seq'=64] {'batch','seq'}, dimensions={0} | all-to-all | bytes 786432 | tf_op jit(solution)/shard_map/all_to_all | solution.py:298
  69.1 0.1 turn.1.own_ref
  69.2 0.7 collective-permute-start
  69.8 0.8 %finish.1 = bf16[1,256,256]{2,1,0:T(8,128)(2,1)} custom-call(f32[768,128]{1,0:T(8,128)S(1)} %bitcast.12), custom_call_target="tpu_custom_call" | custom-call | flops 1000000000 | bytes 1000000 | tf_op jit(solution)/shard_map/finish/pallas_call | solution.py:244
  70.6 0.2 collective-permute-done.other_ref
  70.8 0.7 join.1
  (1 shorter events, 0.0 us)
Async XLA Ops:
  0.6 1.1 %copy-start.1 = (f32[256]{0:T(256)S(1)}, f32[256]{0:T(256)}, u32[]{:S(2)}) copy-start(f32[256]{0:T(256)} %param.7) | copy-start | bytes 3076
  0.6 1.1 %copy-start = (f32[256,256]{1,0:T(8,128)S(1)}, f32[256,256]{1,0:T(8,128)}, u32[]{:S(2)}) copy-start(f32[256,256]{1,0:T(8,128)} %taps_ref.1) | copy-start | bytes 786436
  69.2 1.7 %collective-permute-start = (f32[128,256]{1,0:T(8,128)S(1)}, f32[128,256]{1,0:T(8,128)S(1)}, u32[]{:S(2)}, u32[]{:S(2)}) collective-permute-start(f32[128,256]{1,0:T(8,128)S(1)} %turn.1.own_ref), channel_id=1, source_target_pairs={{0,64},{64,0},{128,192},{192,128},{1,65},{65,1},{129,193},{193,129... | collective-permute-start | bytes 393224 | tf_op jit(solution)/shard_map/ppermute | solution.py:301

commit v9 on v8

--- a/solution.py
+++ b/solution.py
@@ -26,11 +26,15 @@
         rows = slice(half * LANES, (half + 1) * LANES)
         sent_ref[pl.ds(half, channels, stride=SENT), :] = signal_ref[rows, :].T
         sent_ref[pl.ds(HALVES + half, channels, stride=SENT), :] = grad_ref[rows, :].T
-    first = pl.multiple_of(lax.axis_index("batch") * per_batch, per_batch)
-    taps = taps_ref[pl.ds(first, per_batch), :]
-    sent_ref[pl.ds(SENT - 1, channels, stride=SENT), :] = jnp.concatenate(
-        [taps, gain_ref[...]], axis=0
-    ).T
+    b = lax.axis_index("batch")
+    taps = taps_ref[pl.ds(pl.multiple_of(b * per_batch, per_batch), per_batch), :]
+    row = lax.broadcasted_iota(jnp.int32, (LANES, channels), 0)
+    last = jnp.where(
+        row // per_batch == lax.rem(b, LANES // per_batch),
+        jnp.concatenate([taps, taps], axis=0),
+        jnp.concatenate([gain_ref[...], gain_ref[...]], axis=0),
+    )
+    sent_ref[pl.ds(SENT - 1, channels, stride=SENT), :] = last.T
 
 
 def pieces_to_send(signal_rows, grad_rows, filter_taps, gain, per_batch):
@@ -136,12 +140,9 @@
                     total[b, parity, half, 0:height, :] += high[:, lanes] + low[:, lanes]
 
     build(0, 0, even)
-    pieces = LANES // per_batch
+    lower = lax.broadcasted_iota(jnp.int32, (blocks, LANES), 1) < per_batch
     taps = [
-        jnp.concatenate(
-            [rows_of(half * pieces + piece, SENT - 1)[:, :per_batch] for piece in range(pieces)],
-            axis=1,
-        )
+        jnp.where(lower, rows_of(2 * half, SENT - 1), rows_of(2 * half + 1, SENT - 1))
         for half in range(HALVES)
     ]
     high = [half.astype(jnp.bfloat16).astype(jnp.float32) for half in taps]

time: 71.7 us -> 71.7 us (level)
  no operation moved by 1% of the time
where the time goes in v9:
time: 71.7 us; the launch traced here: 71.5 us
  blocking collectives  61.7 us (86%)
  Pallas kernels  7.22 us (10%)
  other arithmetic  1.05 us (1%)
    all_to_all x1, blocking collectives, shards(): got = lax.all_to_all(sent, axes, 0, 0, tiled=True)  38.3 us
    all_to_all x1, blocking collectives, shards(): lax.all_to_all(back.reshape(channels, BACK, 1, LANES), axes, 0, 0, tiled=...  23.4 us
    pallas_call x1, Pallas kernels, correlations(): pl.pallas_call(functools.partial(correlate, batch, blocks), out_shape=jax...  5.41 us
  transfers between devices with their start and end apart: 1, of which 1 were waited for; matrix products, arithmetic and copies ran while one was open for 0% of the time, Pallas kernels for 1%

profile of v9, /device:TPU:1, one launch (start us, length us, event | category | flops | bytes accessed | tf_op | source)
XLA Modules:
  0.0 71.5 jit_solution(18204393684129910561)
XLA Ops:
  0.6 0.0 copy-start.1
  0.6 0.0 copy-start
  0.7 1.0 %bitcast_convert_fusion = (f32[256,256]{1,0:T(8,128)S(1)}, f32[256,256]{1,0:T(8,128)S(1)}) fusion(bf16[1,256,256]{2,1,0:T(8,128)(2,1)} %param.5, bf16[1,256,256]{2,1,0:T(8,128)(2,1)} %param.4), kind=kLoop, calls=%fused_computation | loop fusion | flops 131072 | bytes 786432 | tf_op jit(solution)/shard_map/convert_element_type | solution.py:290
  1.7 0.0 copy-done.1
  1.7 0.0 copy-done
  1.7 0.2 send.1
  2.0 38.3 %all_to_all.10 = f32[256,5,1,128]{3,2,1,0:T(1,128)S(1)} all-to-all(f32[256,5,1,128]{3,2,1,0:T(1,128)S(1)} %bitcast.10), channel_id=1, replica_groups=mesh['batch'=4,'seq'=64] {'batch','seq'}, dimensions={0} | all-to-all | bytes 1310720 | tf_op jit(solution)/shard_map/all_to_all | solution.py:297
  40.3 5.4 %correlate.1 = f32[768,128]{1,0:T(8,128)S(1)} custom-call(f32[1280,128]{1,0:T(8,128)S(1)} %bitcast.13), custom_call_target="tpu_custom_call" | custom-call | flops 6000000000 | bytes 2000000 | tf_op jit(solution)/shard_map/correlate/pallas_call | solution.py:186
  45.7 23.4 %all_to_all.11 = f32[256,3,1,128]{3,2,1,0:T(1,128)S(1)} all-to-all(f32[256,3,1,128]{3,2,1,0:T(1,128)S(1)} %bitcast.14), channel_id=1, replica_groups=mesh['batch'=4,'seq'=64] {'batch','seq'}, dimensions={0} | all-to-all | bytes 786432 | tf_op jit(solution)/shard_map/all_to_all | solution.py:299
  69.0 0.1 turn.1.own_ref
  69.1 0.7 collective-permute-start
  69.8 0.8 %finish.1 = bf16[1,256,256]{2,1,0:T(8,128)(2,1)} custom-call(f32[768,128]{1,0:T(8,128)S(1)} %bitcast.12), custom_call_target="tpu_custom_call" | custom-call | flops 1000000000 | bytes 1000000 | tf_op jit(solution)/shard_map/finish/pallas_call | solution.py:245
  70.6 0.2 collective-permute-done.other_ref
  70.8 0.7 join.1
  (1 shorter events, 0.0 us)
Async XLA Ops:
  0.6 1.1 %copy-start.1 = (f32[256]{0:T(256)S(1)}, f32[256]{0:T(256)}, u32[]{:S(2)}) copy-start(f32[256]{0:T(256)} %param.7) | copy-start | bytes 3076
  0.6 1.1 %copy-start = (f32[256,256]{1,0:T(8,128)S(1)}, f32[256,256]{1,0:T(8,128)}, u32[]{:S(2)}) copy-start(f32[256,256]{1,0:T(8,128)} %taps_ref.1) | copy-start | bytes 786436
  69.1 1.7 %collective-permute-start = (f32[128,256]{1,0:T(8,128)S(1)}, f32[128,256]{1,0:T(8,128)S(1)}, u32[]{:S(2)}, u32[]{:S(2)}) collective-permute-start(f32[128,256]{1,0:T(8,128)S(1)} %turn.1.own_ref), channel_id=1, source_target_pairs={{0,64},{64,0},{128,192},{192,128},{1,65},{65,1},{129,193},{193,129... | collective-permute-start | bytes 393224 | tf_op jit(solution)/shard_map/ppermute | solution.py:302
